TPU v7x, 256 devices: a whole 4x4x8 slice. The times are simulated.
256 devices in a mesh: band: 4 (over x), pulse: 16 (over y, z_lo, core), range: 4 (over z_hi).
Axes of the slice: x: 4, y: 4, z: 8 (z_hi: 4, z_lo: 2; z = z_hi * 2 + z_lo), core: 2. Of those that a mesh axis runs over, the one named last changes fastest.
Arguments:
- echoes: bfloat16 [4, 2, 8192, 4096], P('band', None, 'pulse', 'range'), may hold values from -6 to 6
- range_phase: float32 [4, 4096], P('band'), may hold values from -3.140625 to 3.140625
- pulse_shift: int32 [4, 8192], P('band', ('pulse', 'range')), may hold values from -64 to 64
- bin_offset: int32 [4], replicated, may hold values from 0 to 1024, as said below
- doppler_phase: float32 [8192], replicated, may hold values from -3.140625 to 3.140625
Outputs:
- focused: bfloat16 [12288, 2, 8192], P(('band', 'pulse', 'range'))
Inputs may be any that keep to these rules, and one draw needn't show every extreme that they name: Band b's spectrum begins at combined bin b * 3072 - 2 * 512 + bin_offset[b]. In every draw some band other than the last has offset 2 * 512 and the band after it has offset 0.
All inputs are finite; a program needn't handle non-finite values.
Results may differ from a plain program's by a relative error of at most 0.0054.
Values may be sent and summed in bfloat16 or wider, within the bound.
No kernel may reach another device: no remote copies, remote signals or barrier semaphores. Data moves between devices by JAX's collectives and lax.ppermute only.
A program may use at most 64 MiB of HBM per device.

v0:
```python
import functools
import math

import jax
import jax.numpy as jnp
import ml_dtypes
import numpy as np
from jax import lax
from jax.experimental import pallas as pl
from jax.experimental.pallas import tpu as pltpu
from jax.sharding import PartitionSpec as P


MARGIN = 512
LANES = 128
CHUNKS = 2
F32 = jnp.float32
BF16 = jnp.bfloat16


def split_const(table):
    high = table.astype(ml_dtypes.bfloat16)
    low = (table - high.astype(np.float64)).astype(ml_dtypes.bfloat16)
    return high, low


def unit_roots(rows, cols, modulus, sign):
    product = np.outer(np.arange(rows), np.arange(cols)) % modulus
    angle = sign * 2.0 * np.pi * product / modulus
    return np.cos(angle), np.sin(angle)


def dot_f32(lhs, rhs, contract):
    return lax.dot_general(lhs, rhs, (contract, ((), ())), preferred_element_type=F32)


def complex_mul(a, b):
    return a[0] * b[0] - a[1] * b[1], a[0] * b[1] + a[1] * b[0]


def by_constant(a, angle):
    cos = math.cos(angle)
    sin = math.sin(angle)
    quarter = angle / (math.pi / 2)
    if abs(quarter - round(quarter)) < 1e-9:
        turn = int(round(quarter)) % 4
        if turn == 0:
            return a
        if turn == 1:
            return -a[1], a[0]
        if turn == 2:
            return -a[0], -a[1]
        return a[1], -a[0]
    if abs(abs(cos) - abs(sin)) < 1e-9:
        half = math.sqrt(0.5)
        plus = (a[0] + a[1]) * half
        minus = (a[0] - a[1]) * half
        if cos > 0 and sin > 0:
            return minus, plus
        if cos < 0 and sin > 0:
            return -plus, minus
        if cos < 0 and sin < 0:
            return -minus, -plus
        return plus, -minus
    return a[0] * cos - a[1] * sin, a[0] * sin + a[1] * cos


def small_dft(values, sign):
    count = len(values)
    if count == 1:
        return values
    even = small_dft(values[0::2], sign)
    odd = small_dft(values[1::2], sign)
    first = []
    second = []
    for i in range(count // 2):
        turned = by_constant(odd[i], sign * 2.0 * math.pi * i / count)
        first.append((even[i][0] + turned[0], even[i][1] + turned[1]))
        second.append((even[i][0] - turned[0], even[i][1] - turned[1]))
    return first + second


def turned_rows(product, lanes, rows, at, near_ref, far_ref, phase_ref):
    span = rows.stop - rows.start
    total = product[:2 * span, lanes] + product[2 * span:, lanes]
    near = (near_ref[0, at:at + 1, :], near_ref[1, at:at + 1, :])
    far = (far_ref[0, rows, :], far_ref[1, rows, :])
    phase = (phase_ref[0, at, rows, :], phase_ref[1, at, rows, :])
    return complex_mul((total[:span], total[span:]), complex_mul(complex_mul(far, near), phase))


def ordered_rows(out_ref, order_ref, width):
    pitch = width + 8
    for n in range(out_ref.shape[0] // width):
        out_ref[n * width:(n + 1) * width, :] = (
            order_ref[n * pitch:n * pitch + width, :].astype(BF16))


def cells_kernel(outer, sub, sources, first, scalar_ref, mine_ref, *refs):
    echo_refs = (mine_ref,) + refs[:sources - 1]
    (twist_ref, near_ref, far_ref, phase_ref, table_ref, _, data_ref, spill_ref,
     stage_ref, mid_ref, order_ref) = refs[sources - 1:]
    rows = echo_refs[0].shape[1]
    inner = outer // sources
    group = 16

    def block(t, carry):
        at = pl.multiple_of(t * group, group)
        for n in range(inner):
            lanes = slice(n * LANES, (n + 1) * LANES)
            values = []
            for echo_ref in echo_refs:
                values.append((
                    echo_ref[0, pl.ds(at, group), lanes].astype(F32),
                    echo_ref[1, pl.ds(at, group), lanes].astype(F32),
                ))
            for q, value in enumerate(small_dft(values, -1.0)):
                value = by_constant(value, -2.0 * math.pi * n * q / outer)
                mid_ref[q, n, 0] = value[0]
                mid_ref[q, n, 1] = value[1]
        for q in range(sources):
            values = [(mid_ref[q, n, 0], mid_ref[q, n, 1]) for n in range(inner)]
            for m, value in enumerate(small_dft(values, -1.0)):
                stage_ref[q + sources * m, 0, pl.ds(at, group), :] = value[0]
                stage_ref[q + sources * m, 1, pl.ds(at, group), :] = value[1]
        return carry

    lax.fori_loop(0, rows // group, block, 0)
    shift = scalar_ref[0]
    steps = outer // sub
    pitch = 2 * steps + 8
    kept = slice(first, LANES)
    count = LANES - first
    for step in range(0, steps, 2):
        parts = []
        for i in range(2):
            halves = []
            for h in range(sub):
                bin_low = (step + i) * sub + h
                source = lax.rem(bin_low - shift + 2 * outer, outer)
                twist = (twist_ref[0, bin_low:bin_low + 1, :], twist_ref[1, bin_low:bin_low + 1, :])
                value = complex_mul((stage_ref[source, 0], stage_ref[source, 1]), twist)
                halves.append(jnp.concatenate(value, axis=1).astype(BF16))
            part = jnp.concatenate(halves, axis=0)
            data_ref[step + i] = part
            parts.append(part)
        product = dot_f32(table_ref[...], jnp.concatenate(parts, axis=0), ((1,), (1,)))
        for i in range(2):
            at = step + i
            lanes = slice(i * LANES, (i + 1) * LANES)
            value = turned_rows(product, lanes, kept, at, near_ref, far_ref, phase_ref)
            order_ref[pl.ds(2 * at, count, stride=pitch), :] = value[0]
            order_ref[pl.ds(2 * at + 1, count, stride=pitch), :] = value[1]
    ordered_rows(spill_ref, order_ref, 2 * steps)


def owned_kernel(data_ref, near_ref, far_ref, phase_ref, table_ref, out_ref, order_ref):
    steps = data_ref.shape[0]
    pitch = 2 * steps + 8
    count = table_ref.shape[0] // 4
    kept = slice(0, count)
    for step in range(0, steps, 2):
        data = jnp.concatenate((data_ref[step], data_ref[step + 1]), axis=0)
        product = dot_f32(table_ref[...], data, ((1,), (1,)))
        for i in range(2):
            at = step + i
            lanes = slice(i * LANES, (i + 1) * LANES)
            value = turned_rows(product, lanes, kept, at, near_ref, far_ref, phase_ref)
            order_ref[pl.ds(2 * at, count, stride=pitch), :] = value[0]
            order_ref[pl.ds(2 * at + 1, count, stride=pitch), :] = value[1]
    ordered_rows(out_ref, order_ref, 2 * steps)


def range_tables(first):
    cos, sin = unit_roots(LANES, LANES, LANES, -1.0)
    table = np.zeros((2, LANES, 2, LANES))
    table[0, :, 0], table[0, :, 1] = cos, -sin
    table[1, :, 0], table[1, :, 1] = sin, cos
    stack = lambda part: np.concatenate(split_const(part.reshape(-1, 2 * LANES)))
    return stack(table[:, :first]), stack(table[:, first:])


def cells_stage(scalars, echoes, chunk, received, twist, near, far, phase, gate, sub, first):
    sources = len(received) + 1
    outer = twist.shape[1]
    steps = outer // sub
    table = jnp.asarray(range_tables(first)[1])
    rows = echoes.shape[3]
    whole = lambda shape: pl.BlockSpec(shape, lambda i, s: (0,) * len(shape))
    mine = pl.BlockSpec((2, None, None) + echoes.shape[3:], lambda i, s: (0, s[1], chunk, 0, 0))
    operands = (*received, twist, near, far, phase, table)
    data = jax.ShapeDtypeStruct((steps, LANES, 2 * LANES), BF16)
    spill = jax.ShapeDtypeStruct((2 * steps * (LANES - first), LANES), BF16)
    return pl.pallas_call(
        functools.partial(cells_kernel, outer, sub, sources, first),
        grid_spec=pltpu.PrefetchScalarGridSpec(
            num_scalar_prefetch=1,
            grid=(1,),
            in_specs=[mine, *[whole(value.shape) for value in operands],
                      pl.BlockSpec(memory_space=pl.ANY)],
            out_specs=[whole(data.shape), whole(spill.shape)],
            scratch_shapes=[
                pltpu.VMEM((outer, 2, rows, LANES), F32),
                pltpu.VMEM((sources, outer // sources, 2, 16, LANES), F32),
                pltpu.VMEM(((LANES - first) * (2 * steps + 8), LANES), F32),
            ],
        ),
        out_shape=[data, spill],
        compiler_params=pltpu.CompilerParams(
            dimension_semantics=("arbitrary",), vmem_limit_bytes=16 * 1024 * 1024),
        name="cells_stage",
    )(scalars, echoes, *operands, gate)


def owned_stage(data, near, far, phase, first):
    steps = data.shape[0]
    table = jnp.asarray(range_tables(first)[0])
    vmem = pl.BlockSpec(memory_space=pltpu.VMEM)
    return pl.pallas_call(
        owned_kernel,
        in_specs=[vmem] * 5,
        out_specs=vmem,
        out_shape=jax.ShapeDtypeStruct((2 * steps * first, LANES), BF16),
        scratch_shapes=[pltpu.VMEM((first * (2 * steps + 8), LANES), F32)],
        compiler_params=pltpu.CompilerParams(vmem_limit_bytes=12 * 1024 * 1024),
        name="owned_stage",
    )(data, near, far, phase, table)


def stitch_kernel(sub, scalar_ref, own_ref, low_ref, high_ref, out_ref, first_ref, last_ref, sems):
    height = low_ref.shape[0]
    last = own_ref.shape[0] - height
    lane = lax.broadcasted_iota(jnp.int32, low_ref.shape, 1)
    row = lax.broadcasted_iota(jnp.int32, low_ref.shape, 0)
    index = row // 2 * sub + lane // (LANES // sub)
    middle = pltpu.make_async_copy(
        own_ref.at[height:last], out_ref.at[height:last], sems.at[0])
    middle.start()
    added = jnp.where(index < scalar_ref[2], low_ref[...].astype(F32), 0.0)
    first_ref[...] = (own_ref[:height].astype(F32) + added).astype(BF16)
    begin = pltpu.make_async_copy(first_ref, out_ref.at[:height], sems.at[1])
    begin.start()
    added = jnp.where(index >= scalar_ref[3], high_ref[...].astype(F32), 0.0)
    last_ref[...] = (own_ref[last:].astype(F32) + added).astype(BF16)
    end = pltpu.make_async_copy(last_ref, out_ref.at[last:], sems.at[2])
    end.start()
    middle.wait()
    begin.wait()
    end.wait()


def stitch(scalars, own, from_below, from_above, sub):
    vmem = pl.BlockSpec(memory_space=pltpu.VMEM)
    return pl.pallas_call(
        functools.partial(stitch_kernel, sub),
        in_specs=[pl.BlockSpec(memory_space=pltpu.SMEM), vmem, vmem, vmem],
        out_specs=pl.BlockSpec(memory_space=pl.ANY),
        out_shape=jax.ShapeDtypeStruct(own.shape, BF16),
        scratch_shapes=[pltpu.VMEM(from_below.shape, BF16), pltpu.VMEM(from_below.shape, BF16),
                        pltpu.SemaphoreType.DMA((3,))],
        compiler_params=pltpu.CompilerParams(vmem_limit_bytes=8 * 1024 * 1024),
        name="stitch",
    )(scalars, own, from_below, from_above)


def azimuth_kernel(outer, first_ref, fore_ref, twist_ref, filter_ref, back_ref, last_ref, *refs):
    data_refs = refs[:-1]
    out_ref = refs[-1]
    chunks = len(data_refs)
    width = LANES // chunks
    count = data_refs[0].shape[0]
    twist = (twist_ref[0], twist_ref[1])
    twist_back = (twist_ref[0], -twist_ref[1])
    turn = (filter_ref[0], filter_ref[1])
    left = ((1,), (0,))
    two = lambda lhs, rhs: dot_f32(lhs[0], rhs, left) + dot_f32(lhs[1], rhs, left)
    rows = []
    for c in range(count):
        data = [ref[c] for ref in data_refs]
        spread = two((first_ref[0], first_ref[1]), jnp.concatenate(data, axis=1))
        for h in range(chunks):
            pieces = [spread[:, q * LANES + h * width:q * LANES + (h + 1) * width]
                      for q in range(chunks)]
            joined = jnp.concatenate(pieces, axis=1)
            value = complex_mul((joined[:outer], joined[outer:]), twist)
            rows.append(jnp.concatenate(value, axis=1).astype(BF16))
    total = count * chunks
    stacked = jnp.concatenate(rows, axis=0)
    doppler = dot_f32(stacked, fore_ref[0], left) + dot_f32(stacked, fore_ref[1], left)
    rows = []
    for c in range(total):
        part = doppler[c * outer:(c + 1) * outer]
        value = complex_mul((part[:, :LANES], part[:, LANES:]), turn)
        rows.append(jnp.concatenate(value, axis=1).astype(BF16))
    stacked = jnp.concatenate(rows, axis=0)
    image = dot_f32(stacked, back_ref[0], left) + dot_f32(stacked, back_ref[1], left)
    for c in range(0, total, 2):
        values = []
        for d in range(2):
            part = image[(c + d) * outer:(c + d + 1) * outer]
            value = complex_mul((part[:, :LANES], part[:, LANES:]), twist_back)
            values.append(jnp.concatenate(value, axis=0).astype(BF16))
        value = two((last_ref[0], last_ref[1]), jnp.concatenate(values, axis=1)).astype(BF16)
        out_ref[c] = value[:, :LANES]
        out_ref[c + 1] = value[:, LANES:]


def azimuth_tables(outer):
    cos, sin = unit_roots(outer, outer, outer, -1.0)
    first = np.zeros((2, outer, outer, 2))
    first[0, :, :, 0], first[0, :, :, 1] = cos, -sin
    first[1, :, :, 0], first[1, :, :, 1] = sin, cos
    last = np.zeros((outer, 2, 2, outer))
    last[:, 0, 0], last[:, 0, 1] = cos, sin
    last[:, 1, 0], last[:, 1, 1] = -sin, cos
    cos, sin = unit_roots(LANES, LANES, LANES, -1.0)
    fore = np.zeros((2, LANES, 2, LANES))
    fore[0, :, 0], fore[0, :, 1] = cos, sin
    fore[1, :, 0], fore[1, :, 1] = -sin, cos
    back = np.zeros((2, LANES, 2, LANES))
    back[0, :, 0], back[0, :, 1] = cos, -sin
    back[1, :, 0], back[1, :, 1] = sin, cos
    pair = lambda table, shape: np.stack(split_const(table.reshape(shape)))
    twist = np.stack(unit_roots(outer, LANES, outer * LANES, -1.0)).astype(np.float32)
    square = (2 * LANES, 2 * LANES)
    side = (2 * outer, 2 * outer)
    return pair(first, side), pair(fore, square), twist, pair(back, square), pair(last, side)


def azimuth_stage(data, turn, outer):
    chunks = len(data)
    count = data[0].shape[0]
    block = 16 // chunks
    first, fore, twist, back, last = azimuth_tables(outer)
    whole = lambda shape: pl.BlockSpec(shape, lambda i: (0,) * len(shape))
    tile = pl.BlockSpec((block,) + data[0].shape[1:], lambda i: (i, 0, 0))
    out_shape = (count * chunks,) + data[0].shape[1:]
    return pl.pallas_call(
        functools.partial(azimuth_kernel, outer),
        grid=(count // block,),
        in_specs=[whole(first.shape), whole(fore.shape), whole(twist.shape), whole(turn.shape),
                  whole(back.shape), whole(last.shape)] + [tile] * chunks,
        out_specs=pl.BlockSpec((block * chunks,) + out_shape[1:], lambda i: (i, 0, 0)),
        out_shape=jax.ShapeDtypeStruct(out_shape, BF16),
        compiler_params=pltpu.CompilerParams(
            dimension_semantics=("arbitrary",), vmem_limit_bytes=16 * 1024 * 1024),
        name="azimuth_stage",
    )(jnp.asarray(first), jnp.asarray(fore), jnp.asarray(twist), turn, jnp.asarray(back),
      jnp.asarray(last), *data)


def shifted(block, distance):
    devices = range(lax.axis_size("band"))
    route = [(i - distance, i) for i in devices if i - distance in devices]
    return lax.ppermute(block, "band", route)


def body(echoes, range_phase, pulse_shift, bin_offset, doppler_phase):
    range_count = lax.axis_size("range")
    group_size = lax.axis_size("pulse") * range_count
    cells_local = echoes.shape[3]
    cell_count = cells_local * range_count
    n_local = echoes.shape[2] // range_count
    spill_len = 2 * MARGIN
    owned_bins = cell_count - spill_len
    bins_local = owned_bins // group_size
    outer = cell_count // LANES
    sub = CHUNKS
    piece = n_local // sub
    steps = outer // sub

    band = lax.axis_index("band")
    bands = bin_offset.shape[0]
    order = jnp.arange(bands, dtype=jnp.int32)
    offset_of = lambda index: jnp.sum(jnp.where(order == index, bin_offset, 0))
    offset = offset_of(band)
    below = offset_of(band - 1)
    above = offset_of(band + 1)
    shift = offset - spill_len

    place = lax.axis_index("range")
    low = jnp.arange(outer, dtype=jnp.int32)
    lane = jnp.arange(LANES, dtype=jnp.int32)
    phase = jnp.concatenate((range_phase[0], range_phase[0]))
    phase = lax.dynamic_slice_in_dim(phase, spill_len - offset, cell_count, 0)
    phase = lax.optimization_barrier(jnp.transpose(phase.reshape(LANES, outer)))
    scale = 1.0 / math.sqrt(cell_count)
    phase = phase.reshape(steps, sub, LANES)
    part = lane // piece
    cube = (steps, LANES, LANES)
    spread = []
    for value in (jnp.cos(phase) * scale, jnp.sin(phase) * scale):
        wide = jnp.broadcast_to(value[:, sub - 1][..., None], cube)
        for h in range(sub - 1):
            wide = jnp.where(part == h, value[:, h][..., None], wide)
        spread.append(wide)
    spread = jnp.stack(spread)
    low_bin = jnp.arange(steps, dtype=jnp.int32)[:, None] * sub + part - shift

    def ramp(product):
        angle = jnp.mod(product, cell_count).astype(F32) * (-2.0 * math.pi / cell_count)
        return jnp.stack((jnp.cos(angle), jnp.sin(angle)))

    doppler = jnp.transpose(doppler_phase.reshape(LANES, group_size))
    factor = 1.0 / doppler_phase.shape[0]
    turn = jnp.stack((jnp.cos(doppler) * factor, jnp.sin(doppler) * factor))

    received = []
    source = echoes[0]
    for q in range(sub):
        blocks = []
        for d in range(range_count - 1, 0, -1):
            begin = jnp.mod(place + d, range_count) * n_local + q * piece
            block = lax.dynamic_slice_in_dim(source, begin, piece, 1)
            route = [(i, (i + d) % range_count) for i in range(range_count)]
            blocks.append(lax.ppermute(block, "range", route))
            if d == 1:
                source = lax.optimization_barrier(source)
        received.append(blocks)
    held = echoes[0].reshape(2, range_count, sub, piece, cells_local)
    scalars = jnp.stack((shift, place, below, above))

    twist = ramp((low[:, None] - shift) * (lane[None, :] + cells_local * place))
    samples = []
    gate = None
    for q in range(sub):
        shifts = jnp.tile(pulse_shift[0, q * piece:(q + 1) * piece], sub)
        near = ramp(low_bin * shifts)
        far = ramp(outer * lane[:, None] * shifts)
        gate = twist if gate is None else gate
        first = owned_bins // outer
        data, spill = cells_stage(scalars, held, q, received[q], twist, near, far, spread,
                                  gate, sub, first)
        own = owned_stage(data, near, far, spread, first)
        from_below = shifted(spill, 1)
        from_above = shifted(spill, -1)
        gate = stitch(scalars, own, from_below, from_above, sub)
        blocks = gate.reshape(group_size, bins_local // sub, 2, LANES)
        block = lax.all_to_all(
            blocks, ("pulse", "range"), split_axis=0, concat_axis=0, tiled=True)
        samples.append(jnp.transpose(block, (1, 0, 2, 3)).reshape(
            bins_local // sub, 2 * group_size, LANES))

    image = azimuth_stage(samples, turn, group_size)
    image = jnp.transpose(image.reshape(bins_local, group_size, 2, LANES), (0, 2, 1, 3))
    return image.reshape(bins_local, 2, group_size * LANES)


def solution(mesh):
    in_specs = (
        P("band", None, "pulse", "range"),
        P("band", None),
        P("band", ("pulse", "range")),
        P(),
        P(),
    )
    out_specs = P(("band", "pulse", "range"), None, None)
    return jax.shard_map(
        body, mesh=mesh, in_specs=in_specs, out_specs=out_specs, check_vma=False)
```

profile of v0, /device:TPU:2, one launch (start us, length us, event | category | flops | bytes accessed | tf_op | source)
XLA Modules:
  0.0 159.1 jit_solution(10296141260013362633)
XLA Ops:
  0.0 2.0 %dynamic-slice_bitcast_fusion = (bf16[2,64,1024]{2,1,0:T(8,128)(2,1)S(1)}, bf16[2,64,1024]{2,1,0:T(8,128)(2,1)}, bf16[2,64,1024]{2,1,0:T(8,128)(2,1)}) fusion(bf16[1,2,512,1024]{3,2,1,0:T(8,128)(2,1)} %param.14, s32[]{:T(128)S(6)} %select_n.175, s32[]{:T(128)S(6)} %select_n.173, s32[]{:T(128)S(6)} %select_n.171), kind=kLoop, calls=%fused_computation.3 | loop fusion | bytes 1572876 | tf_op jit(solution)/shard_map/dynamic_slice | solution.py:414
  2.0 6.3 %collective-permute-start = (bf16[2,64,1024]{2,1,0:T(8,128)(2,1)}, bf16[2,64,1024]{2,1,0:T(8,128)(2,1)S(1)}, u32[]{:S(2)}, u32[]{:S(2)}) collective-permute-start(bf16[2,64,1024]{2,1,0:T(8,128)(2,1)} %get-tuple-element.21), channel_id=1, source_target_pairs={{0,3},{1,0},{2,1},{3,2},{4,7},{5,4},{6,5},{7,6},{8,11},{9,8},{10,9... | collective-permute-start | bytes 786440 | tf_op jit(solution)/shard_map/ppermute | solution.py:416
  9.2 2.9 %collective-permute-start.2 = (bf16[2,64,1024]{2,1,0:T(8,128)(2,1)S(1)}, bf16[2,64,1024]{2,1,0:T(8,128)(2,1)S(1)}, u32[]{:S(2)}, u32[]{:S(2)}) collective-permute-start(bf16[2,64,1024]{2,1,0:T(8,128)(2,1)S(1)} %get-tuple-element.19), channel_id=1, source_target_pairs={{0,1},{1,2},{2,3},{3,0},{4,5},{5,6},{6,7},{7,4},{8,9},{9,10},{10,1... | collective-permute-start | bytes 786440 | tf_op jit(solution)/shard_map/ppermute | solution.py:416
  12.1 1.4 fusion.26
  17.3 1.2 fusion.7
  18.8 1.1 broadcast_select_fusion.1
  20.0 1.3 pad_add_fusion.scalar_ref
  21.5 9.5 %collective-permute-done.refs_0_ = bf16[2,64,1024]{2,1,0:T(8,128)(2,1)S(1)} collective-permute-done((bf16[2,64,1024]{2,1,0:T(8,128)(2,1)}, bf16[2,64,1024]{2,1,0:T(8,128)(2,1)S(1)}, u32[]{:S(2)}, u32[]{:S(2)}) %collective-permute-start) | collective-permute-done | bytes 262176 | tf_op jit(solution)/shard_map/ppermute | solution.py:416
  31.1 1.9 %cells_stage.2 = (bf16[16,128,256]{2,1,0:T(8,128)(2,1)S(1)}, bf16[1024,128]{1,0:T(8,128)(2,1)S(1)}) custom-call(s32[4]{0:T(128)S(1)} %pad_add_fusion.scalar_ref, bf16[2,4,2,64,1024]{4,3,2,1,0:T(8,128)(2,1)S(1)} %bitcast.42, bf16[2,64,1024]{2,1,0:T(8,128)(2,1)S(1)} %collective-permute-done.refs_0_, bf16[2,64,1024]{2,1,0:T(8,128)(2,1)S(1)} %collective-permute-done.1.refs_1_, ...), custom_call_target="tpu_custom_call" | custom-call | tf_op jit(solution)/shard_map/cells_stage/pallas_call | solution.py:194
  33.0 3.4 %collective-permute-start.3 = (bf16[1024,128]{1,0:T(8,128)(2,1)S(1)}, bf16[1024,128]{1,0:T(8,128)(2,1)S(1)}, u32[]{:S(2)}, u32[]{:S(2)}) collective-permute-start(bf16[1024,128]{1,0:T(8,128)(2,1)S(1)} %get-tuple-element.10), channel_id=1, source_target_pairs={{0,64},{64,128},{128,192},{1,65},{65,129},{129,193},{2,66},{66,130... | collective-permute-start | bytes 786440 | tf_op jit(solution)/shard_map/ppermute | solution.py:355
  36.4 2.5 %collective-permute-start.4 = (bf16[1024,128]{1,0:T(8,128)(2,1)S(1)}, bf16[1024,128]{1,0:T(8,128)(2,1)S(1)}, u32[]{:S(2)}, u32[]{:S(2)}) collective-permute-start(bf16[1024,128]{1,0:T(8,128)(2,1)S(1)} %get-tuple-element.10), channel_id=1, source_target_pairs={{64,0},{128,64},{192,128},{65,1},{129,65},{193,129},{66,2},{130,66... | collective-permute-start | bytes 786440 | tf_op jit(solution)/shard_map/ppermute | solution.py:355
  39.8 1.4 collective-permute-done.3.low_ref
  41.2 3.4 %collective-permute-done.4.high_ref = bf16[1024,128]{1,0:T(8,128)(2,1)S(1)} collective-permute-done((bf16[1024,128]{1,0:T(8,128)(2,1)S(1)}, bf16[1024,128]{1,0:T(8,128)(2,1)S(1)}, u32[]{:S(2)}, u32[]{:S(2)}) %collective-permute-start.4) | collective-permute-done | bytes 262176 | tf_op jit(solution)/shard_map/ppermute | solution.py:355
  44.6 1.5 stitch.2.refs_8_
  46.2 13.9 %all-to-all-start = ((bf16[64,24,2,128]{3,2,1,0:T(2,128)(2,1)}), bf16[64,24,2,128]{3,2,1,0:T(2,128)(2,1)S(1)}, u32[]{:S(2)}, u32[]{:S(2)}) async-start(bf16[64,24,2,128]{3,2,1,0:T(2,128)(2,1)} %bitcast.21), calls=%async_computation | async-start | bytes 1572864 | tf_op jit(solution)/shard_map/all_to_all | solution.py:439
  60.1 1.2 constant_dynamic-slice_fusion
  61.3 3.8 %collective-permute-start.5 = (bf16[2,64,1024]{2,1,0:T(8,128)(2,1)S(1)}, bf16[2,64,1024]{2,1,0:T(8,128)(2,1)S(1)}, u32[]{:S(2)}, u32[]{:S(2)}) collective-permute-start(bf16[2,64,1024]{2,1,0:T(8,128)(2,1)S(1)} %get-tuple-element.18), channel_id=1, source_target_pairs={{0,3},{1,0},{2,1},{3,2},{4,7},{5,4},{6,5},{7,6},{8,11},{9,8},{10,9... | collective-permute-start | bytes 786440 | tf_op jit(solution)/shard_map/ppermute | solution.py:416
  65.1 2.4 %collective-permute-start.6 = (bf16[2,64,1024]{2,1,0:T(8,128)(2,1)S(1)}, bf16[2,64,1024]{2,1,0:T(8,128)(2,1)S(1)}, u32[]{:S(2)}, u32[]{:S(2)}) collective-permute-start(bf16[2,64,1024]{2,1,0:T(8,128)(2,1)S(1)} %get-tuple-element.17), channel_id=1, source_target_pairs={{0,2},{1,3},{2,0},{3,1},{4,6},{5,7},{6,4},{7,5},{8,10},{9,11},{10,... | collective-permute-start | bytes 786440 | tf_op jit(solution)/shard_map/ppermute | solution.py:416
  67.4 2.4 %collective-permute-start.7 = (bf16[2,64,1024]{2,1,0:T(8,128)(2,1)S(1)}, bf16[2,64,1024]{2,1,0:T(8,128)(2,1)S(1)}, u32[]{:S(2)}, u32[]{:S(2)}) collective-permute-start(bf16[2,64,1024]{2,1,0:T(8,128)(2,1)S(1)} %get-tuple-element.16), channel_id=1, source_target_pairs={{0,1},{1,2},{2,3},{3,0},{4,5},{5,6},{6,7},{7,4},{8,9},{9,10},{10,1... | collective-permute-start | bytes 786440 | tf_op jit(solution)/shard_map/ppermute | solution.py:416
  69.8 23.6 %collective-permute-done.5.refs_0_ = bf16[2,64,1024]{2,1,0:T(8,128)(2,1)S(1)} collective-permute-done((bf16[2,64,1024]{2,1,0:T(8,128)(2,1)S(1)}, bf16[2,64,1024]{2,1,0:T(8,128)(2,1)S(1)}, u32[]{:S(2)}, u32[]{:S(2)}) %collective-permute-start.5) | collective-permute-done | bytes 262176 | tf_op jit(solution)/shard_map/ppermute | solution.py:416
  93.4 6.9 %collective-permute-done.6.refs_1_ = bf16[2,64,1024]{2,1,0:T(8,128)(2,1)S(1)} collective-permute-done((bf16[2,64,1024]{2,1,0:T(8,128)(2,1)S(1)}, bf16[2,64,1024]{2,1,0:T(8,128)(2,1)S(1)}, u32[]{:S(2)}, u32[]{:S(2)}) %collective-permute-start.6) | collective-permute-done | bytes 262176 | tf_op jit(solution)/shard_map/ppermute | solution.py:416
  100.3 3.5 %collective-permute-done.7.refs_2_ = bf16[2,64,1024]{2,1,0:T(8,128)(2,1)S(1)} collective-permute-done((bf16[2,64,1024]{2,1,0:T(8,128)(2,1)S(1)}, bf16[2,64,1024]{2,1,0:T(8,128)(2,1)S(1)}, u32[]{:S(2)}, u32[]{:S(2)}) %collective-permute-start.7) | collective-permute-done | bytes 262176 | tf_op jit(solution)/shard_map/ppermute | solution.py:416
  103.9 1.6 copy-done.1
  105.5 1.9 %cells_stage.3 = (bf16[16,128,256]{2,1,0:T(8,128)(2,1)S(1)}, bf16[1024,128]{1,0:T(8,128)(2,1)S(1)}) custom-call(s32[4]{0:T(128)S(1)} %pad_add_fusion.scalar_ref, bf16[2,4,2,64,1024]{4,3,2,1,0:T(8,128)(2,1)S(1)} %bitcast.43, bf16[2,64,1024]{2,1,0:T(8,128)(2,1)S(1)} %collective-permute-done.5.refs_0_, bf16[2,64,1024]{2,1,0:T(8,128)(2,1)S(1)} %collective-permute-done.6.refs_1_, ...), custom_call_target="tpu_custom_call" | custom-call | tf_op jit(solution)/shard_map/cells_stage/pallas_call | solution.py:194
  107.3 3.1 %collective-permute-start.8 = (bf16[1024,128]{1,0:T(8,128)(2,1)S(1)}, bf16[1024,128]{1,0:T(8,128)(2,1)S(1)}, u32[]{:S(2)}, u32[]{:S(2)}) collective-permute-start(bf16[1024,128]{1,0:T(8,128)(2,1)S(1)} %get-tuple-element.12), channel_id=1, source_target_pairs={{0,64},{64,128},{128,192},{1,65},{65,129},{129,193},{2,66},{66,130... | collective-permute-start | bytes 786440 | tf_op jit(solution)/shard_map/ppermute | solution.py:355
  110.5 2.9 %collective-permute-start.9 = (bf16[1024,128]{1,0:T(8,128)(2,1)S(1)}, bf16[1024,128]{1,0:T(8,128)(2,1)S(1)}, u32[]{:S(2)}, u32[]{:S(2)}) collective-permute-start(bf16[1024,128]{1,0:T(8,128)(2,1)S(1)} %get-tuple-element.12), channel_id=1, source_target_pairs={{64,0},{128,64},{192,128},{65,1},{129,65},{193,129},{66,2},{130,66... | collective-permute-start | bytes 786440 | tf_op jit(solution)/shard_map/ppermute | solution.py:355
  114.4 2.6 %collective-permute-done.8.low_ref = bf16[1024,128]{1,0:T(8,128)(2,1)S(1)} collective-permute-done((bf16[1024,128]{1,0:T(8,128)(2,1)S(1)}, bf16[1024,128]{1,0:T(8,128)(2,1)S(1)}, u32[]{:S(2)}, u32[]{:S(2)}) %collective-permute-start.8) | collective-permute-done | bytes 262176 | tf_op jit(solution)/shard_map/ppermute | solution.py:355
  117.0 2.8 %collective-permute-done.9.high_ref = bf16[1024,128]{1,0:T(8,128)(2,1)S(1)} collective-permute-done((bf16[1024,128]{1,0:T(8,128)(2,1)S(1)}, bf16[1024,128]{1,0:T(8,128)(2,1)S(1)}, u32[]{:S(2)}, u32[]{:S(2)}) %collective-permute-start.9) | collective-permute-done | bytes 262176 | tf_op jit(solution)/shard_map/ppermute | solution.py:355
  119.8 1.5 stitch.3
  121.4 7.6 %all-to-all-start.1 = ((bf16[64,24,2,128]{3,2,1,0:T(2,128)(2,1)}), bf16[64,24,2,128]{3,2,1,0:T(2,128)(2,1)S(1)}, u32[]{:S(2)}, u32[]{:S(2)}) async-start(bf16[64,24,2,128]{3,2,1,0:T(2,128)(2,1)} %bitcast.26), calls=%async_computation.1 | async-start | bytes 1572864 | tf_op jit(solution)/shard_map/all_to_all | solution.py:439
  130.3 22.2 %all-to-all-done.1 = bf16[64,24,2,128]{3,2,1,0:T(2,128)(2,1)S(1)} async-done(((bf16[64,24,2,128]{3,2,1,0:T(2,128)(2,1)}), bf16[64,24,2,128]{3,2,1,0:T(2,128)(2,1)S(1)}, u32[]{:S(2)}, u32[]{:S(2)}) %all-to-all-start.1) | async-done | bytes 786464 | tf_op jit(solution)/shard_map/all_to_all | solution.py:439
  153.3 5.8 %azimuth_stage.1 = bf16[48,128,128]{2,1,0:T(8,128)(2,1)} custom-call(bf16[2,128,128]{2,1,0:T(8,128)(2,1)S(1)} %copy-done.6, bf16[2,256,256]{2,1,0:T(8,128)(2,1)S(1)} %copy-done.4, f32[2,64,128]{2,1,0:T(8,128)S(1)} %copy-done.7, f32[2,64,128]{2,1,0:T(8,128)S(1)} %pad_maximum_fusion.3.filter_ref, bf16[2,256,256]{2,1,0:T(8,128)(2,1)S(1)} %copy-done.5, ...), custom_call_target="tpu_custom_call" | custom-call | tf_op jit(solution)/shard_map/azimuth_stage/pallas_call | solution.py:338
  (60 shorter events, 7.5 us)
Async XLA Ops:
  2.0 29.1 %collective-permute-start = (bf16[2,64,1024]{2,1,0:T(8,128)(2,1)}, bf16[2,64,1024]{2,1,0:T(8,128)(2,1)S(1)}, u32[]{:S(2)}, u32[]{:S(2)}) collective-permute-start(bf16[2,64,1024]{2,1,0:T(8,128)(2,1)} %get-tuple-element.21), channel_id=1, source_target_pairs={{0,3},{1,0},{2,1},{3,2},{4,7},{5,4},{6,5},{7,6},{8,11},{9,8},{10,9... | collective-permute-start | bytes 786440 | tf_op jit(solution)/shard_map/ppermute | solution.py:416
  8.3 22.8 %collective-permute-start.1 = (bf16[2,64,1024]{2,1,0:T(8,128)(2,1)}, bf16[2,64,1024]{2,1,0:T(8,128)(2,1)S(1)}, u32[]{:S(2)}, u32[]{:S(2)}) collective-permute-start(bf16[2,64,1024]{2,1,0:T(8,128)(2,1)} %get-tuple-element.20), channel_id=1, source_target_pairs={{0,2},{1,3},{2,0},{3,1},{4,6},{5,7},{6,4},{7,5},{8,10},{9,11},{10,... | collective-permute-start | bytes 786440 | tf_op jit(solution)/shard_map/ppermute | solution.py:416
  9.2 21.9 %collective-permute-start.2 = (bf16[2,64,1024]{2,1,0:T(8,128)(2,1)S(1)}, bf16[2,64,1024]{2,1,0:T(8,128)(2,1)S(1)}, u32[]{:S(2)}, u32[]{:S(2)}) collective-permute-start(bf16[2,64,1024]{2,1,0:T(8,128)(2,1)S(1)} %get-tuple-element.19), channel_id=1, source_target_pairs={{0,1},{1,2},{2,3},{3,0},{4,5},{5,6},{6,7},{7,4},{8,9},{9,10},{10,1... | collective-permute-start | bytes 786440 | tf_op jit(solution)/shard_map/ppermute | solution.py:416
  21.3 9.7 %copy-start = (bf16[1,2,512,1024]{3,2,1,0:T(8,128)(2,1)S(1)}, bf16[1,2,512,1024]{3,2,1,0:T(8,128)(2,1)}, u32[]{:S(2)}) copy-start(bf16[1,2,512,1024]{3,2,1,0:T(8,128)(2,1)} %param.14) | copy-start | bytes 6291460
  21.3 9.7 %copy-start.3 = (bf16[128,256]{1,0:T(8,128)(2,1)S(1)}, bf16[128,256]{1,0:T(8,128)(2,1)}, u32[]{:S(2)}) copy-start(bf16[128,256]{1,0:T(8,128)(2,1)} %constant.145.clone.refs_7_) | copy-start | bytes 196612
  31.1 7.8 %copy-start.2 = (bf16[384,256]{1,0:T(8,128)(2,1)S(1)}, bf16[384,256]{1,0:T(8,128)(2,1)}, u32[]{:S(2)}) copy-start(bf16[384,256]{1,0:T(8,128)(2,1)} %constant.146.clone.table_ref) | copy-start | bytes 589828
  33.0 8.3 %collective-permute-start.3 = (bf16[1024,128]{1,0:T(8,128)(2,1)S(1)}, bf16[1024,128]{1,0:T(8,128)(2,1)S(1)}, u32[]{:S(2)}, u32[]{:S(2)}) collective-permute-start(bf16[1024,128]{1,0:T(8,128)(2,1)S(1)} %get-tuple-element.10), channel_id=1, source_target_pairs={{0,64},{64,128},{128,192},{1,65},{65,129},{129,193},{2,66},{66,130... | collective-permute-start | bytes 786440 | tf_op jit(solution)/shard_map/ppermute | solution.py:355
  36.4 8.3 %collective-permute-start.4 = (bf16[1024,128]{1,0:T(8,128)(2,1)S(1)}, bf16[1024,128]{1,0:T(8,128)(2,1)S(1)}, u32[]{:S(2)}, u32[]{:S(2)}) collective-permute-start(bf16[1024,128]{1,0:T(8,128)(2,1)S(1)} %get-tuple-element.10), channel_id=1, source_target_pairs={{64,0},{128,64},{192,128},{65,1},{129,65},{193,129},{66,2},{130,66... | collective-permute-start | bytes 786440 | tf_op jit(solution)/shard_map/ppermute | solution.py:355
  46.2 23.6 %copy-start.9 = (f32[1,128,128]{2,1,0:T(8,128)S(1)}, f32[1,128,128]{2,1,0:T(8,128)}, u32[]{:S(2)}) copy-start(f32[1,128,128]{2,1,0:T(8,128)} %get-tuple-element.35) | copy-start | bytes 196612
  46.2 75.2 %all-to-all-start = ((bf16[64,24,2,128]{3,2,1,0:T(2,128)(2,1)}), bf16[64,24,2,128]{3,2,1,0:T(2,128)(2,1)S(1)}, u32[]{:S(2)}, u32[]{:S(2)}) async-start(bf16[64,24,2,128]{3,2,1,0:T(2,128)(2,1)} %bitcast.21), calls=%async_computation | async-start | bytes 1572864 | tf_op jit(solution)/shard_map/all_to_all | solution.py:439
  61.3 32.1 %collective-permute-start.5 = (bf16[2,64,1024]{2,1,0:T(8,128)(2,1)S(1)}, bf16[2,64,1024]{2,1,0:T(8,128)(2,1)S(1)}, u32[]{:S(2)}, u32[]{:S(2)}) collective-permute-start(bf16[2,64,1024]{2,1,0:T(8,128)(2,1)S(1)} %get-tuple-element.18), channel_id=1, source_target_pairs={{0,3},{1,0},{2,1},{3,2},{4,7},{5,4},{6,5},{7,6},{8,11},{9,8},{10,9... | collective-permute-start | bytes 786440 | tf_op jit(solution)/shard_map/ppermute | solution.py:416
  65.1 35.3 %collective-permute-start.6 = (bf16[2,64,1024]{2,1,0:T(8,128)(2,1)S(1)}, bf16[2,64,1024]{2,1,0:T(8,128)(2,1)S(1)}, u32[]{:S(2)}, u32[]{:S(2)}) collective-permute-start(bf16[2,64,1024]{2,1,0:T(8,128)(2,1)S(1)} %get-tuple-element.17), channel_id=1, source_target_pairs={{0,2},{1,3},{2,0},{3,1},{4,6},{5,7},{6,4},{7,5},{8,10},{9,11},{10,... | collective-permute-start | bytes 786440 | tf_op jit(solution)/shard_map/ppermute | solution.py:416
  67.4 36.5 %collective-permute-start.7 = (bf16[2,64,1024]{2,1,0:T(8,128)(2,1)S(1)}, bf16[2,64,1024]{2,1,0:T(8,128)(2,1)S(1)}, u32[]{:S(2)}, u32[]{:S(2)}) collective-permute-start(bf16[2,64,1024]{2,1,0:T(8,128)(2,1)S(1)} %get-tuple-element.16), channel_id=1, source_target_pairs={{0,1},{1,2},{2,3},{3,0},{4,5},{5,6},{6,7},{7,4},{8,9},{9,10},{10,1... | collective-permute-start | bytes 786440 | tf_op jit(solution)/shard_map/ppermute | solution.py:416
  103.9 1.6 %copy-start.1 = (bf16[1,2,512,1024]{3,2,1,0:T(8,128)(2,1)S(1)}, bf16[1,2,512,1024]{3,2,1,0:T(8,128)(2,1)}, u32[]{:S(2)}) copy-start(bf16[1,2,512,1024]{3,2,1,0:T(8,128)(2,1)} %param.14) | copy-start | bytes 6291460
  107.3 9.6 %collective-permute-start.8 = (bf16[1024,128]{1,0:T(8,128)(2,1)S(1)}, bf16[1024,128]{1,0:T(8,128)(2,1)S(1)}, u32[]{:S(2)}, u32[]{:S(2)}) collective-permute-start(bf16[1024,128]{1,0:T(8,128)(2,1)S(1)} %get-tuple-element.12), channel_id=1, source_target_pairs={{0,64},{64,128},{128,192},{1,65},{65,129},{129,193},{2,66},{66,130... | collective-permute-start | bytes 786440 | tf_op jit(solution)/shard_map/ppermute | solution.py:355
  110.5 9.4 %collective-permute-start.9 = (bf16[1024,128]{1,0:T(8,128)(2,1)S(1)}, bf16[1024,128]{1,0:T(8,128)(2,1)S(1)}, u32[]{:S(2)}, u32[]{:S(2)}) collective-permute-start(bf16[1024,128]{1,0:T(8,128)(2,1)S(1)} %get-tuple-element.12), channel_id=1, source_target_pairs={{64,0},{128,64},{192,128},{65,1},{129,65},{193,129},{66,2},{130,66... | collective-permute-start | bytes 786440 | tf_op jit(solution)/shard_map/ppermute | solution.py:355
  114.4 14.6 %copy-start.10 = (f32[8192]{0:T(1024)S(1)}, f32[8192]{0:T(1024)}, u32[]{:S(2)}) copy-start(f32[8192]{0:T(1024)} %param.18) | copy-start | bytes 98308
  121.4 31.1 %all-to-all-start.1 = ((bf16[64,24,2,128]{3,2,1,0:T(2,128)(2,1)}), bf16[64,24,2,128]{3,2,1,0:T(2,128)(2,1)S(1)}, u32[]{:S(2)}, u32[]{:S(2)}) async-start(bf16[64,24,2,128]{3,2,1,0:T(2,128)(2,1)} %bitcast.26), calls=%async_computation.1 | async-start | bytes 1572864 | tf_op jit(solution)/shard_map/all_to_all | solution.py:439
  129.0 24.3 %copy-start.4 = (bf16[2,256,256]{2,1,0:T(8,128)(2,1)S(1)}, bf16[2,256,256]{2,1,0:T(8,128)(2,1)}, u32[]{:S(2)}) copy-start(bf16[2,256,256]{2,1,0:T(8,128)(2,1)} %constant.148.clone.fore_ref) | copy-start | bytes 786436
  129.0 24.3 %copy-start.5 = (bf16[2,256,256]{2,1,0:T(8,128)(2,1)S(1)}, bf16[2,256,256]{2,1,0:T(8,128)(2,1)}, u32[]{:S(2)}) copy-start(bf16[2,256,256]{2,1,0:T(8,128)(2,1)} %constant.150.clone.back_ref) | copy-start | bytes 786436
  129.0 24.3 %copy-start.6 = (bf16[2,128,128]{2,1,0:T(8,128)(2,1)S(1)}, bf16[2,128,128]{2,1,0:T(8,128)(2,1)}, u32[]{:S(2)}) copy-start(bf16[2,128,128]{2,1,0:T(8,128)(2,1)} %constant.147.clone.first_ref) | copy-start | bytes 196612
  129.0 24.3 %copy-start.7 = (f32[2,64,128]{2,1,0:T(8,128)S(1)}, f32[2,64,128]{2,1,0:T(8,128)}, u32[]{:S(2)}) copy-start(f32[2,64,128]{2,1,0:T(8,128)} %constant.149.clone.twist_ref) | copy-start | bytes 196612
  129.0 24.3 %copy-start.8 = (bf16[2,128,128]{2,1,0:T(8,128)(2,1)S(1)}, bf16[2,128,128]{2,1,0:T(8,128)(2,1)}, u32[]{:S(2)}) copy-start(bf16[2,128,128]{2,1,0:T(8,128)(2,1)} %constant.151.clone.last_ref) | copy-start | bytes 196612
where the time goes:
time: 161 us; the launch traced here: 159 us
  waiting for transfers between devices  76.1 us (47%)
  starting transfers between devices  51.9 us (32%)
  Pallas kernels  14.5 us (9%)
  local copies, waits for them, and re-layouts  7.8 us (5%)
  other arithmetic  6.7 us (4%)
  between operations  2.04 us (1%)
    ppermute x6, waiting for transfers between devices, body(): blocks.append(lax.ppermute(block, 'range', route))  43.6 us
    all_to_all x2, waiting for transfers between devices, body(): lax.all_to_all(blocks, ('pulse', 'range'), split_axis=0, concat_axis=0, t...  22.2 us
    all_to_all x2, starting transfers between devices, body(): lax.all_to_all(blocks, ('pulse', 'range'), split_axis=0, concat_axis=0, t...  21.4 us
    ppermute x6, starting transfers between devices, body(): blocks.append(lax.ppermute(block, 'range', route))  18.6 us
    ppermute x4, starting transfers between devices, shifted(): return lax.ppermute(block, 'band', route)  11.9 us
    ppermute x4, waiting for transfers between devices, shifted(): return lax.ppermute(block, 'band', route)  10.3 us
    pallas_call x1, Pallas kernels, azimuth_stage(): pl.pallas_call(functools.partial(azimuth_kernel, outer), grid=(count // b...  5.76 us
    pallas_call x2, Pallas kernels, cells_stage(): pl.pallas_call(functools.partial(cells_kernel, outer, sub, sources, first...  3.74 us
  transfers between devices with their start and end apart: 12, of which 9 were waited for; matrix products, arithmetic and copies ran while one was open for 6% of the time, Pallas kernels for 3%

commit v1 on v0

--- a/solution.py
+++ b/solution.py
@@ -227,64 +227,91 @@
     )(data, near, far, phase, table)
 
 
-def stitch_kernel(sub, scalar_ref, own_ref, low_ref, high_ref, out_ref, first_ref, last_ref, sems):
-    height = low_ref.shape[0]
-    last = own_ref.shape[0] - height
-    lane = lax.broadcasted_iota(jnp.int32, low_ref.shape, 1)
-    row = lax.broadcasted_iota(jnp.int32, low_ref.shape, 0)
+def stitch_kernel(sub, scalar_ref, own_ref, low_ref, high_ref, out_ref, held_ref, sems):
+    _, ranges, height, _ = held_ref.shape
+    unit = 16
+    edge = low_ref.shape[0] // unit
+    count = own_ref.shape[0] // unit
+    per_block = height // unit
+    lane = lax.broadcasted_iota(jnp.int32, (unit, LANES), 1)
+    row = lax.broadcasted_iota(jnp.int32, (unit, LANES), 0)
     index = row // 2 * sub + lane // (LANES // sub)
-    middle = pltpu.make_async_copy(
-        own_ref.at[height:last], out_ref.at[height:last], sems.at[0])
-    middle.start()
-    added = jnp.where(index < scalar_ref[2], low_ref[...].astype(F32), 0.0)
-    first_ref[...] = (own_ref[:height].astype(F32) + added).astype(BF16)
-    begin = pltpu.make_async_copy(first_ref, out_ref.at[:height], sems.at[1])
-    begin.start()
-    added = jnp.where(index >= scalar_ref[3], high_ref[...].astype(F32), 0.0)
-    last_ref[...] = (own_ref[last:].astype(F32) + added).astype(BF16)
-    end = pltpu.make_async_copy(last_ref, out_ref.at[last:], sems.at[2])
-    end.start()
-    middle.wait()
-    begin.wait()
-    end.wait()
-
-
-def stitch(scalars, own, from_below, from_above, sub):
+    per_unit = unit // 2 * sub
+    for i in range(count):
+        rows = slice(i * unit, (i + 1) * unit)
+        value = own_ref[rows]
+        if i < edge:
+            added = jnp.where(index < scalar_ref[2] - i * per_unit, low_ref[rows].astype(F32), 0.0)
+            value = (value.astype(F32) + added).astype(BF16)
+        elif i >= count - edge:
+            j = i - (count - edge)
+            other = high_ref[j * unit:(j + 1) * unit].astype(F32)
+            added = jnp.where(index >= scalar_ref[3] - j * per_unit, other, 0.0)
+            value = (value.astype(F32) + added).astype(BF16)
+        block = i // per_block
+        at = i % per_block * unit
+        held_ref[block // ranges, block % ranges, at:at + unit] = value
+    copies = [pltpu.make_async_copy(held_ref.at[:, r], out_ref.at[r], sems.at[r])
+              for r in range(ranges)]
+    for copy in copies:
+        copy.start()
+    for copy in copies:
+        copy.wait()
+
+
+def stitch(scalars, own, from_below, from_above, sub, pulses, ranges):
     vmem = pl.BlockSpec(memory_space=pltpu.VMEM)
+    height = own.shape[0] // (pulses * ranges)
     return pl.pallas_call(
         functools.partial(stitch_kernel, sub),
         in_specs=[pl.BlockSpec(memory_space=pltpu.SMEM), vmem, vmem, vmem],
         out_specs=pl.BlockSpec(memory_space=pl.ANY),
-        out_shape=jax.ShapeDtypeStruct(own.shape, BF16),
-        scratch_shapes=[pltpu.VMEM(from_below.shape, BF16), pltpu.VMEM(from_below.shape, BF16),
-                        pltpu.SemaphoreType.DMA((3,))],
+        out_shape=jax.ShapeDtypeStruct((ranges, pulses, height, LANES), BF16),
+        scratch_shapes=[pltpu.VMEM((pulses, ranges, height, LANES), BF16),
+                        pltpu.SemaphoreType.DMA((ranges,))],
         compiler_params=pltpu.CompilerParams(vmem_limit_bytes=8 * 1024 * 1024),
         name="stitch",
     )(scalars, own, from_below, from_above)
 
 
-def azimuth_kernel(outer, first_ref, fore_ref, twist_ref, filter_ref, back_ref, last_ref, *refs):
-    data_refs = refs[:-1]
-    out_ref = refs[-1]
-    chunks = len(data_refs)
-    width = LANES // chunks
-    count = data_refs[0].shape[0]
+def spread_rows(first_ref, data, twist_ref):
+    left = ((1,), (0,))
+    wide = jnp.concatenate(data, axis=1)
+    spread = dot_f32(first_ref[0], wide, left) + dot_f32(first_ref[1], wide, left)
+    half = spread.shape[0] // 2
     twist = (twist_ref[0], twist_ref[1])
-    twist_back = (twist_ref[0], -twist_ref[1])
+    rows = []
+    for i in range(len(data)):
+        lanes = slice(i * LANES, (i + 1) * LANES)
+        real, imag = complex_mul((spread[:half, lanes], spread[half:, lanes]), twist)
+        width = LANES // CHUNKS
+        for h in range(CHUNKS):
+            part = slice(h * width, (h + 1) * width)
+            rows.append(jnp.concatenate((real[:, part], imag[:, part]), axis=1).astype(BF16))
+    return rows
+
+
+def spread_kernel(first_ref, twist_ref, data_ref, out_ref):
+    for c in range(0, data_ref.shape[0], 2):
+        rows = spread_rows(first_ref, (data_ref[c], data_ref[c + 1]), twist_ref)
+        for i, value in enumerate(rows):
+            out_ref[c * CHUNKS + i] = value
+
+
+def azimuth_kernel(outer, first_ref, fore_ref, twist_ref, back_twist_ref, filter_ref, back_ref,
+                   last_ref, *refs):
+    early_refs = refs[:-2]
+    data_ref, out_ref = refs[-2:]
+    twist_back = (back_twist_ref[0], -back_twist_ref[1])
     turn = (filter_ref[0], filter_ref[1])
     left = ((1,), (0,))
     two = lambda lhs, rhs: dot_f32(lhs[0], rhs, left) + dot_f32(lhs[1], rhs, left)
     rows = []
-    for c in range(count):
-        data = [ref[c] for ref in data_refs]
-        spread = two((first_ref[0], first_ref[1]), jnp.concatenate(data, axis=1))
-        for h in range(chunks):
-            pieces = [spread[:, q * LANES + h * width:q * LANES + (h + 1) * width]
-                      for q in range(chunks)]
-            joined = jnp.concatenate(pieces, axis=1)
-            value = complex_mul((joined[:outer], joined[outer:]), twist)
-            rows.append(jnp.concatenate(value, axis=1).astype(BF16))
-    total = count * chunks
+    for c in range(0, data_ref.shape[0], 2):
+        rows += spread_rows(first_ref, (data_ref[c], data_ref[c + 1]), twist_ref)
+    total = len(rows)
+    rows = [jnp.concatenate([ref[c] for ref in early_refs] + [rows[c]], axis=1)
+            for c in range(total)]
     stacked = jnp.concatenate(rows, axis=0)
     doppler = dot_f32(stacked, fore_ref[0], left) + dot_f32(stacked, fore_ref[1], left)
     rows = []
@@ -305,11 +332,13 @@
         out_ref[c + 1] = value[:, LANES:]
 
 
-def azimuth_tables(outer):
+def azimuth_tables(outer, ranges):
     cos, sin = unit_roots(outer, outer, outer, -1.0)
     first = np.zeros((2, outer, outer, 2))
     first[0, :, :, 0], first[0, :, :, 1] = cos, -sin
     first[1, :, :, 0], first[1, :, :, 1] = sin, cos
+    slots = np.arange(outer)
+    first = first[:, :, slots % (outer // ranges) * ranges + slots // (outer // ranges)]
     last = np.zeros((outer, 2, 2, outer))
     last[:, 0, 0], last[:, 0, 1] = cos, sin
     last[:, 1, 0], last[:, 1, 1] = -sin, cos
@@ -321,32 +350,52 @@
     back[0, :, 0], back[0, :, 1] = cos, -sin
     back[1, :, 0], back[1, :, 1] = sin, cos
     pair = lambda table, shape: np.stack(split_const(table.reshape(shape)))
+    fore = fore.reshape(2, CHUNKS, LANES // CHUNKS, 2 * LANES).transpose(1, 0, 2, 3)
     twist = np.stack(unit_roots(outer, LANES, outer * LANES, -1.0)).astype(np.float32)
     square = (2 * LANES, 2 * LANES)
     side = (2 * outer, 2 * outer)
     return pair(first, side), pair(fore, square), twist, pair(back, square), pair(last, side)
 
 
-def azimuth_stage(data, turn, outer):
-    chunks = len(data)
-    count = data[0].shape[0]
+def chunk_twist(twist, chunk):
+    width = LANES // CHUNKS
+    return jnp.asarray(np.tile(twist[:, :, chunk * width:(chunk + 1) * width], CHUNKS))
+
+
+def spread_stage(data, chunk, outer, ranges):
+    first, _, twist, _, _ = azimuth_tables(outer, ranges)
+    vmem = pl.BlockSpec(memory_space=pltpu.VMEM)
+    return pl.pallas_call(
+        spread_kernel,
+        in_specs=[vmem] * 3,
+        out_specs=vmem,
+        out_shape=jax.ShapeDtypeStruct((data.shape[0] * CHUNKS, outer, LANES), BF16),
+        compiler_params=pltpu.CompilerParams(vmem_limit_bytes=12 * 1024 * 1024),
+        name="spread_stage",
+    )(jnp.asarray(first), chunk_twist(twist, chunk), data)
+
+
+def azimuth_stage(early, data, turn, outer, ranges):
+    chunks = CHUNKS
+    count = data.shape[0]
     block = 16 // chunks
-    first, fore, twist, back, last = azimuth_tables(outer)
+    first, fore, twist, back, last = azimuth_tables(outer, ranges)
+    constants = [jnp.asarray(first), jnp.asarray(fore), chunk_twist(twist, chunks - 1),
+                 jnp.asarray(twist), turn, jnp.asarray(back), jnp.asarray(last)]
     whole = lambda shape: pl.BlockSpec(shape, lambda i: (0,) * len(shape))
-    tile = pl.BlockSpec((block,) + data[0].shape[1:], lambda i: (i, 0, 0))
-    out_shape = (count * chunks,) + data[0].shape[1:]
+    tile = lambda rows, shape: pl.BlockSpec((rows,) + shape[1:], lambda i: (i, 0, 0))
+    out_shape = (count * chunks,) + data.shape[1:]
     return pl.pallas_call(
         functools.partial(azimuth_kernel, outer),
         grid=(count // block,),
-        in_specs=[whole(first.shape), whole(fore.shape), whole(twist.shape), whole(turn.shape),
-                  whole(back.shape), whole(last.shape)] + [tile] * chunks,
-        out_specs=pl.BlockSpec((block * chunks,) + out_shape[1:], lambda i: (i, 0, 0)),
+        in_specs=[whole(value.shape) for value in constants]
+        + [tile(block * chunks, value.shape) for value in early] + [tile(block, data.shape)],
+        out_specs=tile(block * chunks, out_shape),
         out_shape=jax.ShapeDtypeStruct(out_shape, BF16),
         compiler_params=pltpu.CompilerParams(
             dimension_semantics=("arbitrary",), vmem_limit_bytes=16 * 1024 * 1024),
         name="azimuth_stage",
-    )(jnp.asarray(first), jnp.asarray(fore), jnp.asarray(twist), turn, jnp.asarray(back),
-      jnp.asarray(last), *data)
+    )(*constants, *early, data)
 
 
 def shifted(block, distance):
@@ -434,14 +483,16 @@
         own = owned_stage(data, near, far, spread, first)
         from_below = shifted(spill, 1)
         from_above = shifted(spill, -1)
-        gate = stitch(scalars, own, from_below, from_above, sub)
+        gate = stitch(scalars, own, from_below, from_above, sub,
+                      group_size // range_count, range_count)
         blocks = gate.reshape(group_size, bins_local // sub, 2, LANES)
         block = lax.all_to_all(
-            blocks, ("pulse", "range"), split_axis=0, concat_axis=0, tiled=True)
+            blocks, ("range", "pulse"), split_axis=0, concat_axis=0, tiled=True)
         samples.append(jnp.transpose(block, (1, 0, 2, 3)).reshape(
             bins_local // sub, 2 * group_size, LANES))
 
-    image = azimuth_stage(samples, turn, group_size)
+    early = [spread_stage(samples[q], q, group_size, range_count) for q in range(sub - 1)]
+    image = azimuth_stage(early, samples[-1], turn, group_size, range_count)
     image = jnp.transpose(image.reshape(bins_local, group_size, 2, LANES), (0, 2, 1, 3))
     return image.reshape(bins_local, 2, group_size * LANES)
 

time: 161 us -> 162 us (level)
  transfers between devices with their start and end apart: 12 -> 12, of which waited for: 9 -> 9; matrix products, arithmetic and copies ran while one was open for 6% -> 6% of each run, Pallas kernels for 3% -> 4%
where the time goes in v1:
time: 162 us; the launch traced here: 161 us
  waiting for transfers between devices  75.4 us (47%)
  starting transfers between devices  52.1 us (32%)
  Pallas kernels  15.4 us (10%)
  local copies, waits for them, and re-layouts  8.97 us (6%)
  other arithmetic  6.69 us (4%)
  between operations  2.08 us (1%)
    ppermute x6, waiting for transfers between devices, body(): blocks.append(lax.ppermute(block, 'range', route))  43.7 us
    all_to_all x2, starting transfers between devices, body(): lax.all_to_all(blocks, ('range', 'pulse'), split_axis=0, concat_axis=0, t...  21.5 us
    all_to_all x2, waiting for transfers between devices, body(): lax.all_to_all(blocks, ('range', 'pulse'), split_axis=0, concat_axis=0, t...  21.4 us
    ppermute x6, starting transfers between devices, body(): blocks.append(lax.ppermute(block, 'range', route))  18.7 us
    ppermute x4, starting transfers between devices, shifted(): return lax.ppermute(block, 'band', route)  11.9 us
    ppermute x4, waiting for transfers between devices, shifted(): return lax.ppermute(block, 'band', route)  10.3 us
    pallas_call x1, Pallas kernels, azimuth_stage(): pl.pallas_call(functools.partial(azimuth_kernel, outer), grid=(count // b...  5.67 us
    pallas_call x2, Pallas kernels, cells_stage(): pl.pallas_call(functools.partial(cells_kernel, outer, sub, sources, first...  3.74 us
  transfers between devices with their start and end apart: 12, of which 9 were waited for; matrix products, arithmetic and copies ran while one was open for 6% of the time, Pallas kernels for 4%

profile of v1, /device:TPU:2, one launch (start us, length us, event | category | flops | bytes accessed | tf_op | source)
XLA Modules:
  0.0 160.6 jit_solution(7359970617880370936)
XLA Ops:
  0.0 2.0 %dynamic-slice_bitcast_fusion = (bf16[2,64,1024]{2,1,0:T(8,128)(2,1)S(1)}, bf16[2,64,1024]{2,1,0:T(8,128)(2,1)}, bf16[2,64,1024]{2,1,0:T(8,128)(2,1)}) fusion(bf16[1,2,512,1024]{3,2,1,0:T(8,128)(2,1)} %param.17, s32[]{:T(128)S(6)} %select_n.175, s32[]{:T(128)S(6)} %select_n.173, s32[]{:T(128)S(6)} %select_n.171), kind=kLoop, calls=%fused_computation.3 | loop fusion | bytes 1572876 | tf_op jit(solution)/shard_map/dynamic_slice | solution.py:463
  2.0 6.3 %collective-permute-start = (bf16[2,64,1024]{2,1,0:T(8,128)(2,1)}, bf16[2,64,1024]{2,1,0:T(8,128)(2,1)S(1)}, u32[]{:S(2)}, u32[]{:S(2)}) collective-permute-start(bf16[2,64,1024]{2,1,0:T(8,128)(2,1)} %get-tuple-element.21), channel_id=1, source_target_pairs={{0,3},{1,0},{2,1},{3,2},{4,7},{5,4},{6,5},{7,6},{8,11},{9,8},{10,9... | collective-permute-start | bytes 786440 | tf_op jit(solution)/shard_map/ppermute | solution.py:465
  9.2 2.9 %collective-permute-start.2 = (bf16[2,64,1024]{2,1,0:T(8,128)(2,1)S(1)}, bf16[2,64,1024]{2,1,0:T(8,128)(2,1)S(1)}, u32[]{:S(2)}, u32[]{:S(2)}) collective-permute-start(bf16[2,64,1024]{2,1,0:T(8,128)(2,1)S(1)} %get-tuple-element.19), channel_id=1, source_target_pairs={{0,1},{1,2},{2,3},{3,0},{4,5},{5,6},{6,7},{7,4},{8,9},{9,10},{10,1... | collective-permute-start | bytes 786440 | tf_op jit(solution)/shard_map/ppermute | solution.py:465
  12.1 1.4 fusion.26
  17.3 1.2 fusion.7
  20.0 1.3 pad_add_fusion.scalar_ref
  21.5 9.5 %collective-permute-done.refs_0_ = bf16[2,64,1024]{2,1,0:T(8,128)(2,1)S(1)} collective-permute-done((bf16[2,64,1024]{2,1,0:T(8,128)(2,1)}, bf16[2,64,1024]{2,1,0:T(8,128)(2,1)S(1)}, u32[]{:S(2)}, u32[]{:S(2)}) %collective-permute-start) | collective-permute-done | bytes 262176 | tf_op jit(solution)/shard_map/ppermute | solution.py:465
  31.1 1.9 %cells_stage.2 = (bf16[16,128,256]{2,1,0:T(8,128)(2,1)S(1)}, bf16[1024,128]{1,0:T(8,128)(2,1)S(1)}) custom-call(s32[4]{0:T(128)S(1)} %pad_add_fusion.scalar_ref, bf16[2,4,2,64,1024]{4,3,2,1,0:T(8,128)(2,1)S(1)} %bitcast.42, bf16[2,64,1024]{2,1,0:T(8,128)(2,1)S(1)} %collective-permute-done.refs_0_, bf16[2,64,1024]{2,1,0:T(8,128)(2,1)S(1)} %collective-permute-done.1.refs_1_, ...), custom_call_target="tpu_custom_call" | custom-call | tf_op jit(solution)/shard_map/cells_stage/pallas_call | solution.py:194
  32.9 3.4 %collective-permute-start.3 = (bf16[1024,128]{1,0:T(8,128)(2,1)S(1)}, bf16[1024,128]{1,0:T(8,128)(2,1)S(1)}, u32[]{:S(2)}, u32[]{:S(2)}) collective-permute-start(bf16[1024,128]{1,0:T(8,128)(2,1)S(1)} %get-tuple-element.10), channel_id=1, source_target_pairs={{0,64},{64,128},{128,192},{1,65},{65,129},{129,193},{2,66},{66,130... | collective-permute-start | bytes 786440 | tf_op jit(solution)/shard_map/ppermute | solution.py:404
  36.4 2.5 %collective-permute-start.4 = (bf16[1024,128]{1,0:T(8,128)(2,1)S(1)}, bf16[1024,128]{1,0:T(8,128)(2,1)S(1)}, u32[]{:S(2)}, u32[]{:S(2)}) collective-permute-start(bf16[1024,128]{1,0:T(8,128)(2,1)S(1)} %get-tuple-element.10), channel_id=1, source_target_pairs={{64,0},{128,64},{192,128},{65,1},{129,65},{193,129},{66,2},{130,66... | collective-permute-start | bytes 786440 | tf_op jit(solution)/shard_map/ppermute | solution.py:404
  39.8 1.4 collective-permute-done.3.low_ref
  41.2 3.4 %collective-permute-done.4.high_ref = bf16[1024,128]{1,0:T(8,128)(2,1)S(1)} collective-permute-done((bf16[1024,128]{1,0:T(8,128)(2,1)S(1)}, bf16[1024,128]{1,0:T(8,128)(2,1)S(1)}, u32[]{:S(2)}, u32[]{:S(2)}) %collective-permute-start.4) | collective-permute-done | bytes 262176 | tf_op jit(solution)/shard_map/ppermute | solution.py:404
  44.6 1.7 %stitch.2.refs_8_ = bf16[4,16,48,128]{3,2,1,0:T(8,128)(2,1)} custom-call(s32[4]{0:T(128)S(1)} %pad_add_fusion.scalar_ref, bf16[3072,128]{1,0:T(8,128)(2,1)S(1)} %owned_stage.2.own_ref, bf16[1024,128]{1,0:T(8,128)(2,1)S(1)} %collective-permute-done.3.low_ref, bf16[1024,128]{1,0:T(8,128)(2,1)S(1)} %collective-permute-done.4.high_ref), custom_call_target="tpu_custom_call" | custom-call | tf_op jit(solution)/shard_map/stitch/pallas_call | solution.py:265
  46.3 13.9 %all-to-all-start = ((bf16[64,24,2,128]{3,2,1,0:T(2,128)(2,1)}), bf16[64,24,2,128]{3,2,1,0:T(2,128)(2,1)S(1)}, u32[]{:S(2)}, u32[]{:S(2)}) async-start(bf16[64,24,2,128]{3,2,1,0:T(2,128)(2,1)} %bitcast.21), calls=%async_computation | async-start | bytes 1572864 | tf_op jit(solution)/shard_map/all_to_all | solution.py:489
  60.2 1.2 constant_dynamic-slice_fusion
  61.4 4.0 %collective-permute-start.5 = (bf16[2,64,1024]{2,1,0:T(8,128)(2,1)S(1)}, bf16[2,64,1024]{2,1,0:T(8,128)(2,1)S(1)}, u32[]{:S(2)}, u32[]{:S(2)}) collective-permute-start(bf16[2,64,1024]{2,1,0:T(8,128)(2,1)S(1)} %get-tuple-element.18), channel_id=1, source_target_pairs={{0,3},{1,0},{2,1},{3,2},{4,7},{5,4},{6,5},{7,6},{8,11},{9,8},{10,9... | collective-permute-start | bytes 786440 | tf_op jit(solution)/shard_map/ppermute | solution.py:465
  65.4 2.2 %collective-permute-start.6 = (bf16[2,64,1024]{2,1,0:T(8,128)(2,1)S(1)}, bf16[2,64,1024]{2,1,0:T(8,128)(2,1)S(1)}, u32[]{:S(2)}, u32[]{:S(2)}) collective-permute-start(bf16[2,64,1024]{2,1,0:T(8,128)(2,1)S(1)} %get-tuple-element.17), channel_id=1, source_target_pairs={{0,2},{1,3},{2,0},{3,1},{4,6},{5,7},{6,4},{7,5},{8,10},{9,11},{10,... | collective-permute-start | bytes 786440 | tf_op jit(solution)/shard_map/ppermute | solution.py:465
  67.5 2.5 %collective-permute-start.7 = (bf16[2,64,1024]{2,1,0:T(8,128)(2,1)S(1)}, bf16[2,64,1024]{2,1,0:T(8,128)(2,1)S(1)}, u32[]{:S(2)}, u32[]{:S(2)}) collective-permute-start(bf16[2,64,1024]{2,1,0:T(8,128)(2,1)S(1)} %get-tuple-element.16), channel_id=1, source_target_pairs={{0,1},{1,2},{2,3},{3,0},{4,5},{5,6},{6,7},{7,4},{8,9},{9,10},{10,1... | collective-permute-start | bytes 786440 | tf_op jit(solution)/shard_map/ppermute | solution.py:465
  70.0 22.9 %collective-permute-done.5.refs_0_ = bf16[2,64,1024]{2,1,0:T(8,128)(2,1)S(1)} collective-permute-done((bf16[2,64,1024]{2,1,0:T(8,128)(2,1)S(1)}, bf16[2,64,1024]{2,1,0:T(8,128)(2,1)S(1)}, u32[]{:S(2)}, u32[]{:S(2)}) %collective-permute-start.5) | collective-permute-done | bytes 262176 | tf_op jit(solution)/shard_map/ppermute | solution.py:465
  92.9 7.6 %collective-permute-done.6.refs_1_ = bf16[2,64,1024]{2,1,0:T(8,128)(2,1)S(1)} collective-permute-done((bf16[2,64,1024]{2,1,0:T(8,128)(2,1)S(1)}, bf16[2,64,1024]{2,1,0:T(8,128)(2,1)S(1)}, u32[]{:S(2)}, u32[]{:S(2)}) %collective-permute-start.6) | collective-permute-done | bytes 262176 | tf_op jit(solution)/shard_map/ppermute | solution.py:465
  100.5 3.7 %collective-permute-done.7.refs_2_ = bf16[2,64,1024]{2,1,0:T(8,128)(2,1)S(1)} collective-permute-done((bf16[2,64,1024]{2,1,0:T(8,128)(2,1)S(1)}, bf16[2,64,1024]{2,1,0:T(8,128)(2,1)S(1)}, u32[]{:S(2)}, u32[]{:S(2)}) %collective-permute-start.7) | collective-permute-done | bytes 262176 | tf_op jit(solution)/shard_map/ppermute | solution.py:465
  104.2 1.6 copy-done.1
  105.8 1.9 %cells_stage.3 = (bf16[16,128,256]{2,1,0:T(8,128)(2,1)S(1)}, bf16[1024,128]{1,0:T(8,128)(2,1)S(1)}) custom-call(s32[4]{0:T(128)S(1)} %pad_add_fusion.scalar_ref, bf16[2,4,2,64,1024]{4,3,2,1,0:T(8,128)(2,1)S(1)} %bitcast.43, bf16[2,64,1024]{2,1,0:T(8,128)(2,1)S(1)} %collective-permute-done.5.refs_0_, bf16[2,64,1024]{2,1,0:T(8,128)(2,1)S(1)} %collective-permute-done.6.refs_1_, ...), custom_call_target="tpu_custom_call" | custom-call | tf_op jit(solution)/shard_map/cells_stage/pallas_call | solution.py:194
  107.7 3.1 %collective-permute-start.8 = (bf16[1024,128]{1,0:T(8,128)(2,1)S(1)}, bf16[1024,128]{1,0:T(8,128)(2,1)S(1)}, u32[]{:S(2)}, u32[]{:S(2)}) collective-permute-start(bf16[1024,128]{1,0:T(8,128)(2,1)S(1)} %get-tuple-element.12), channel_id=1, source_target_pairs={{0,64},{64,128},{128,192},{1,65},{65,129},{129,193},{2,66},{66,130... | collective-permute-start | bytes 786440 | tf_op jit(solution)/shard_map/ppermute | solution.py:404
  110.8 2.9 %collective-permute-start.9 = (bf16[1024,128]{1,0:T(8,128)(2,1)S(1)}, bf16[1024,128]{1,0:T(8,128)(2,1)S(1)}, u32[]{:S(2)}, u32[]{:S(2)}) collective-permute-start(bf16[1024,128]{1,0:T(8,128)(2,1)S(1)} %get-tuple-element.12), channel_id=1, source_target_pairs={{64,0},{128,64},{192,128},{65,1},{129,65},{193,129},{66,2},{130,66... | collective-permute-start | bytes 786440 | tf_op jit(solution)/shard_map/ppermute | solution.py:404
  114.7 2.6 %collective-permute-done.8.low_ref = bf16[1024,128]{1,0:T(8,128)(2,1)S(1)} collective-permute-done((bf16[1024,128]{1,0:T(8,128)(2,1)S(1)}, bf16[1024,128]{1,0:T(8,128)(2,1)S(1)}, u32[]{:S(2)}, u32[]{:S(2)}) %collective-permute-start.8) | collective-permute-done | bytes 262176 | tf_op jit(solution)/shard_map/ppermute | solution.py:404
  117.3 2.8 %collective-permute-done.9.high_ref = bf16[1024,128]{1,0:T(8,128)(2,1)S(1)} collective-permute-done((bf16[1024,128]{1,0:T(8,128)(2,1)S(1)}, bf16[1024,128]{1,0:T(8,128)(2,1)S(1)}, u32[]{:S(2)}, u32[]{:S(2)}) %collective-permute-start.9) | collective-permute-done | bytes 262176 | tf_op jit(solution)/shard_map/ppermute | solution.py:404
  120.2 1.7 %stitch.3 = bf16[4,16,48,128]{3,2,1,0:T(8,128)(2,1)} custom-call(s32[4]{0:T(128)S(1)} %pad_add_fusion.scalar_ref, bf16[3072,128]{1,0:T(8,128)(2,1)S(1)} %owned_stage.3.own_ref, bf16[1024,128]{1,0:T(8,128)(2,1)S(1)} %collective-permute-done.8.low_ref, bf16[1024,128]{1,0:T(8,128)(2,1)S(1)} %collective-permute-done.9.high_ref), custom_call_target="tpu_custom_call" | custom-call | tf_op jit(solution)/shard_map/stitch/pallas_call | solution.py:265
  121.9 7.6 %all-to-all-start.1 = ((bf16[64,24,2,128]{3,2,1,0:T(2,128)(2,1)}), bf16[64,24,2,128]{3,2,1,0:T(2,128)(2,1)}, u32[]{:S(2)}, u32[]{:S(2)}) async-start(bf16[64,24,2,128]{3,2,1,0:T(2,128)(2,1)} %bitcast.26), calls=%async_computation.1 | async-start | bytes 1572864 | tf_op jit(solution)/shard_map/all_to_all | solution.py:489
  131.6 21.4 %all-to-all-done.1 = bf16[64,24,2,128]{3,2,1,0:T(2,128)(2,1)} async-done(((bf16[64,24,2,128]{3,2,1,0:T(2,128)(2,1)}), bf16[64,24,2,128]{3,2,1,0:T(2,128)(2,1)}, u32[]{:S(2)}, u32[]{:S(2)}) %all-to-all-start.1) | async-done | bytes 786464 | tf_op jit(solution)/shard_map/all_to_all | solution.py:489
  153.0 1.9 %copy.39 = bf16[24,64,2,128]{3,2,1,0:T(2,128)(2,1)S(1)} copy(bf16[24,64,2,128]{3,2,0,1:T(2,128)(2,1)} %bitcast.27) | data formatting | bytes 1572864 | tf_op jit(solution)/shard_map/transpose | solution.py:491
  154.9 5.7 %azimuth_stage.1 = bf16[48,128,128]{2,1,0:T(8,128)(2,1)} custom-call(bf16[2,128,128]{2,1,0:T(8,128)(2,1)S(1)} %copy-done.4, bf16[2,256,256]{2,1,0:T(8,128)(2,1)S(1)} %copy-done.5, f32[2,64,128]{2,1,0:T(8,128)S(1)} %copy-done.7, f32[2,64,128]{2,1,0:T(8,128)S(1)} %copy-done.8, f32[2,64,128]{2,1,0:T(8,128)S(1)} %pad_maximum_fusion.3.filter_ref, ...), custom_call_target="tpu_custom_call" | custom-call | tf_op jit(solution)/shard_map/azimuth_stage/pallas_call | solution.py:388
  (65 shorter events, 8.5 us)
Async XLA Ops:
  2.0 29.1 %collective-permute-start = (bf16[2,64,1024]{2,1,0:T(8,128)(2,1)}, bf16[2,64,1024]{2,1,0:T(8,128)(2,1)S(1)}, u32[]{:S(2)}, u32[]{:S(2)}) collective-permute-start(bf16[2,64,1024]{2,1,0:T(8,128)(2,1)} %get-tuple-element.21), channel_id=1, source_target_pairs={{0,3},{1,0},{2,1},{3,2},{4,7},{5,4},{6,5},{7,6},{8,11},{9,8},{10,9... | collective-permute-start | bytes 786440 | tf_op jit(solution)/shard_map/ppermute | solution.py:465
  8.3 22.8 %collective-permute-start.1 = (bf16[2,64,1024]{2,1,0:T(8,128)(2,1)}, bf16[2,64,1024]{2,1,0:T(8,128)(2,1)S(1)}, u32[]{:S(2)}, u32[]{:S(2)}) collective-permute-start(bf16[2,64,1024]{2,1,0:T(8,128)(2,1)} %get-tuple-element.20), channel_id=1, source_target_pairs={{0,2},{1,3},{2,0},{3,1},{4,6},{5,7},{6,4},{7,5},{8,10},{9,11},{10,... | collective-permute-start | bytes 786440 | tf_op jit(solution)/shard_map/ppermute | solution.py:465
  9.2 21.9 %collective-permute-start.2 = (bf16[2,64,1024]{2,1,0:T(8,128)(2,1)S(1)}, bf16[2,64,1024]{2,1,0:T(8,128)(2,1)S(1)}, u32[]{:S(2)}, u32[]{:S(2)}) collective-permute-start(bf16[2,64,1024]{2,1,0:T(8,128)(2,1)S(1)} %get-tuple-element.19), channel_id=1, source_target_pairs={{0,1},{1,2},{2,3},{3,0},{4,5},{5,6},{6,7},{7,4},{8,9},{9,10},{10,1... | collective-permute-start | bytes 786440 | tf_op jit(solution)/shard_map/ppermute | solution.py:465
  21.3 9.7 %copy-start = (bf16[1,2,512,1024]{3,2,1,0:T(8,128)(2,1)S(1)}, bf16[1,2,512,1024]{3,2,1,0:T(8,128)(2,1)}, u32[]{:S(2)}) copy-start(bf16[1,2,512,1024]{3,2,1,0:T(8,128)(2,1)} %param.17) | copy-start | bytes 6291460
  21.3 9.7 %copy-start.3 = (bf16[128,256]{1,0:T(8,128)(2,1)S(1)}, bf16[128,256]{1,0:T(8,128)(2,1)}, u32[]{:S(2)}) copy-start(bf16[128,256]{1,0:T(8,128)(2,1)} %constant.149.clone.refs_7_) | copy-start | bytes 196612
  31.1 7.8 %copy-start.2 = (bf16[384,256]{1,0:T(8,128)(2,1)S(1)}, bf16[384,256]{1,0:T(8,128)(2,1)}, u32[]{:S(2)}) copy-start(bf16[384,256]{1,0:T(8,128)(2,1)} %constant.150.clone.table_ref) | copy-start | bytes 589828
  32.9 8.3 %collective-permute-start.3 = (bf16[1024,128]{1,0:T(8,128)(2,1)S(1)}, bf16[1024,128]{1,0:T(8,128)(2,1)S(1)}, u32[]{:S(2)}, u32[]{:S(2)}) collective-permute-start(bf16[1024,128]{1,0:T(8,128)(2,1)S(1)} %get-tuple-element.10), channel_id=1, source_target_pairs={{0,64},{64,128},{128,192},{1,65},{65,129},{129,193},{2,66},{66,130... | collective-permute-start | bytes 786440 | tf_op jit(solution)/shard_map/ppermute | solution.py:404
  36.4 8.3 %collective-permute-start.4 = (bf16[1024,128]{1,0:T(8,128)(2,1)S(1)}, bf16[1024,128]{1,0:T(8,128)(2,1)S(1)}, u32[]{:S(2)}, u32[]{:S(2)}) collective-permute-start(bf16[1024,128]{1,0:T(8,128)(2,1)S(1)} %get-tuple-element.10), channel_id=1, source_target_pairs={{64,0},{128,64},{192,128},{65,1},{129,65},{193,129},{66,2},{130,66... | collective-permute-start | bytes 786440 | tf_op jit(solution)/shard_map/ppermute | solution.py:404
  46.3 23.7 %copy-start.11 = (f32[1,128,128]{2,1,0:T(8,128)S(1)}, f32[1,128,128]{2,1,0:T(8,128)}, u32[]{:S(2)}) copy-start(f32[1,128,128]{2,1,0:T(8,128)} %get-tuple-element.35) | copy-start | bytes 196612
  46.3 75.6 %all-to-all-start = ((bf16[64,24,2,128]{3,2,1,0:T(2,128)(2,1)}), bf16[64,24,2,128]{3,2,1,0:T(2,128)(2,1)S(1)}, u32[]{:S(2)}, u32[]{:S(2)}) async-start(bf16[64,24,2,128]{3,2,1,0:T(2,128)(2,1)} %bitcast.21), calls=%async_computation | async-start | bytes 1572864 | tf_op jit(solution)/shard_map/all_to_all | solution.py:489
  61.4 31.5 %collective-permute-start.5 = (bf16[2,64,1024]{2,1,0:T(8,128)(2,1)S(1)}, bf16[2,64,1024]{2,1,0:T(8,128)(2,1)S(1)}, u32[]{:S(2)}, u32[]{:S(2)}) collective-permute-start(bf16[2,64,1024]{2,1,0:T(8,128)(2,1)S(1)} %get-tuple-element.18), channel_id=1, source_target_pairs={{0,3},{1,0},{2,1},{3,2},{4,7},{5,4},{6,5},{7,6},{8,11},{9,8},{10,9... | collective-permute-start | bytes 786440 | tf_op jit(solution)/shard_map/ppermute | solution.py:465
  65.4 35.1 %collective-permute-start.6 = (bf16[2,64,1024]{2,1,0:T(8,128)(2,1)S(1)}, bf16[2,64,1024]{2,1,0:T(8,128)(2,1)S(1)}, u32[]{:S(2)}, u32[]{:S(2)}) collective-permute-start(bf16[2,64,1024]{2,1,0:T(8,128)(2,1)S(1)} %get-tuple-element.17), channel_id=1, source_target_pairs={{0,2},{1,3},{2,0},{3,1},{4,6},{5,7},{6,4},{7,5},{8,10},{9,11},{10,... | collective-permute-start | bytes 786440 | tf_op jit(solution)/shard_map/ppermute | solution.py:465
  67.5 36.7 %collective-permute-start.7 = (bf16[2,64,1024]{2,1,0:T(8,128)(2,1)S(1)}, bf16[2,64,1024]{2,1,0:T(8,128)(2,1)S(1)}, u32[]{:S(2)}, u32[]{:S(2)}) collective-permute-start(bf16[2,64,1024]{2,1,0:T(8,128)(2,1)S(1)} %get-tuple-element.16), channel_id=1, source_target_pairs={{0,1},{1,2},{2,3},{3,0},{4,5},{5,6},{6,7},{7,4},{8,9},{9,10},{10,1... | collective-permute-start | bytes 786440 | tf_op jit(solution)/shard_map/ppermute | solution.py:465
  104.2 1.6 copy-start.1
  107.7 9.6 %collective-permute-start.8 = (bf16[1024,128]{1,0:T(8,128)(2,1)S(1)}, bf16[1024,128]{1,0:T(8,128)(2,1)S(1)}, u32[]{:S(2)}, u32[]{:S(2)}) collective-permute-start(bf16[1024,128]{1,0:T(8,128)(2,1)S(1)} %get-tuple-element.12), channel_id=1, source_target_pairs={{0,64},{64,128},{128,192},{1,65},{65,129},{129,193},{2,66},{66,130... | collective-permute-start | bytes 786440 | tf_op jit(solution)/shard_map/ppermute | solution.py:404
  110.8 9.4 %collective-permute-start.9 = (bf16[1024,128]{1,0:T(8,128)(2,1)S(1)}, bf16[1024,128]{1,0:T(8,128)(2,1)S(1)}, u32[]{:S(2)}, u32[]{:S(2)}) collective-permute-start(bf16[1024,128]{1,0:T(8,128)(2,1)S(1)} %get-tuple-element.12), channel_id=1, source_target_pairs={{64,0},{128,64},{192,128},{65,1},{129,65},{193,129},{66,2},{130,66... | collective-permute-start | bytes 786440 | tf_op jit(solution)/shard_map/ppermute | solution.py:404
  114.7 14.8 %copy-start.12 = (f32[8192]{0:T(1024)S(1)}, f32[8192]{0:T(1024)}, u32[]{:S(2)}) copy-start(f32[8192]{0:T(1024)} %param.21) | copy-start | bytes 98308
  121.9 9.0 %copy-start.4 = (bf16[2,128,128]{2,1,0:T(8,128)(2,1)S(1)}, bf16[2,128,128]{2,1,0:T(8,128)(2,1)}, u32[]{:S(2)}) copy-start(bf16[2,128,128]{2,1,0:T(8,128)(2,1)} %constant.151.clone.first_ref) | copy-start | bytes 196612
  121.9 9.0 %copy-start.10 = (f32[2,64,128]{2,1,0:T(8,128)S(1)}, f32[2,64,128]{2,1,0:T(8,128)}, u32[]{:S(2)}) copy-start(f32[2,64,128]{2,1,0:T(8,128)} %constant.152.clone.twist_ref) | copy-start | bytes 196612
  121.9 31.0 %all-to-all-start.1 = ((bf16[64,24,2,128]{3,2,1,0:T(2,128)(2,1)}), bf16[64,24,2,128]{3,2,1,0:T(2,128)(2,1)}, u32[]{:S(2)}, u32[]{:S(2)}) async-start(bf16[64,24,2,128]{3,2,1,0:T(2,128)(2,1)} %bitcast.26), calls=%async_computation.1 | async-start | bytes 1572864 | tf_op jit(solution)/shard_map/all_to_all | solution.py:489
  130.0 24.9 %copy-start.5 = (bf16[2,256,256]{2,1,0:T(8,128)(2,1)S(1)}, bf16[2,256,256]{2,1,0:T(8,128)(2,1)}, u32[]{:S(2)}) copy-start(bf16[2,256,256]{2,1,0:T(8,128)(2,1)} %constant.153.clone.fore_ref) | copy-start | bytes 786436
  130.0 24.9 %copy-start.6 = (bf16[2,256,256]{2,1,0:T(8,128)(2,1)S(1)}, bf16[2,256,256]{2,1,0:T(8,128)(2,1)}, u32[]{:S(2)}) copy-start(bf16[2,256,256]{2,1,0:T(8,128)(2,1)} %constant.156.clone.back_ref) | copy-start | bytes 786436
  130.0 24.9 %copy-start.7 = (f32[2,64,128]{2,1,0:T(8,128)S(1)}, f32[2,64,128]{2,1,0:T(8,128)}, u32[]{:S(2)}) copy-start(f32[2,64,128]{2,1,0:T(8,128)} %constant.154.clone.twist_ref) | copy-start | bytes 196612
  130.0 24.9 %copy-start.8 = (f32[2,64,128]{2,1,0:T(8,128)S(1)}, f32[2,64,128]{2,1,0:T(8,128)}, u32[]{:S(2)}) copy-start(f32[2,64,128]{2,1,0:T(8,128)} %constant.155.clone.back_twist_ref) | copy-start | bytes 196612
  130.1 24.9 %copy-start.9 = (bf16[2,128,128]{2,1,0:T(8,128)(2,1)S(1)}, bf16[2,128,128]{2,1,0:T(8,128)(2,1)}, u32[]{:S(2)}) copy-start(bf16[2,128,128]{2,1,0:T(8,128)(2,1)} %constant.157.clone.last_ref) | copy-start | bytes 196612

commit v2 on v1

--- a/solution.py
+++ b/solution.py
@@ -28,6 +28,12 @@
     product = np.outer(np.arange(rows), np.arange(cols)) % modulus
     angle = sign * 2.0 * np.pi * product / modulus
     return np.cos(angle), np.sin(angle)
+
+
+def split_value(value):
+    high = value.astype(BF16)
+    low = (value - high.astype(F32)).astype(BF16)
+    return high, low
 
 
 def dot_f32(lhs, rhs, contract):
@@ -80,9 +86,15 @@
     return first + second
 
 
+def bin_rows(table_ref, high, low):
+    span = table_ref.shape[0] // 2
+    product = dot_f32(table_ref[...], high, ((1,), (1,)))
+    return product[:span] + product[span:] + dot_f32(table_ref[:span], low, ((1,), (1,)))
+
+
 def turned_rows(product, lanes, rows, at, near_ref, far_ref, phase_ref):
     span = rows.stop - rows.start
-    total = product[:2 * span, lanes] + product[2 * span:, lanes]
+    total = product[:, lanes]
     near = (near_ref[0, at:at + 1, :], near_ref[1, at:at + 1, :])
     far = (far_ref[0, rows, :], far_ref[1, rows, :])
     phase = (phase_ref[0, at, rows, :], phase_ref[1, at, rows, :])
@@ -140,11 +152,13 @@
                 source = lax.rem(bin_low - shift + 2 * outer, outer)
                 twist = (twist_ref[0, bin_low:bin_low + 1, :], twist_ref[1, bin_low:bin_low + 1, :])
                 value = complex_mul((stage_ref[source, 0], stage_ref[source, 1]), twist)
-                halves.append(jnp.concatenate(value, axis=1).astype(BF16))
-            part = jnp.concatenate(halves, axis=0)
-            data_ref[step + i] = part
+                halves.append(jnp.concatenate(value, axis=1))
+            part = split_value(jnp.concatenate(halves, axis=0))
+            data_ref[0, step + i] = part[0]
+            data_ref[1, step + i] = part[1]
             parts.append(part)
-        product = dot_f32(table_ref[...], jnp.concatenate(parts, axis=0), ((1,), (1,)))
+        product = bin_rows(table_ref, jnp.concatenate([part[0] for part in parts], axis=0),
+                           jnp.concatenate([part[1] for part in parts], axis=0))
         for i in range(2):
             at = step + i
             lanes = slice(i * LANES, (i + 1) * LANES)
@@ -155,13 +169,13 @@
 
 
 def owned_kernel(data_ref, near_ref, far_ref, phase_ref, table_ref, out_ref, order_ref):
-    steps = data_ref.shape[0]
+    steps = data_ref.shape[1]
     pitch = 2 * steps + 8
     count = table_ref.shape[0] // 4
     kept = slice(0, count)
     for step in range(0, steps, 2):
-        data = jnp.concatenate((data_ref[step], data_ref[step + 1]), axis=0)
-        product = dot_f32(table_ref[...], data, ((1,), (1,)))
+        product = bin_rows(table_ref, *[
+            jnp.concatenate((data_ref[n, step], data_ref[n, step + 1]), axis=0) for n in range(2)])
         for i in range(2):
             at = step + i
             lanes = slice(i * LANES, (i + 1) * LANES)
@@ -189,7 +203,7 @@
     whole = lambda shape: pl.BlockSpec(shape, lambda i, s: (0,) * len(shape))
     mine = pl.BlockSpec((2, None, None) + echoes.shape[3:], lambda i, s: (0, s[1], chunk, 0, 0))
     operands = (*received, twist, near, far, phase, table)
-    data = jax.ShapeDtypeStruct((steps, LANES, 2 * LANES), BF16)
+    data = jax.ShapeDtypeStruct((2, steps, LANES, 2 * LANES), BF16)
     spill = jax.ShapeDtypeStruct((2 * steps * (LANES - first), LANES), BF16)
     return pl.pallas_call(
         functools.partial(cells_kernel, outer, sub, sources, first),
@@ -213,7 +227,7 @@
 
 
 def owned_stage(data, near, far, phase, first):
-    steps = data.shape[0]
+    steps = data.shape[1]
     table = jnp.asarray(range_tables(first)[0])
     vmem = pl.BlockSpec(memory_space=pltpu.VMEM)
     return pl.pallas_call(
@@ -313,14 +327,14 @@
     rows = [jnp.concatenate([ref[c] for ref in early_refs] + [rows[c]], axis=1)
             for c in range(total)]
     stacked = jnp.concatenate(rows, axis=0)
-    doppler = dot_f32(stacked, fore_ref[0], left) + dot_f32(stacked, fore_ref[1], left)
+    doppler = dot_f32(stacked, fore_ref[...], left)
     rows = []
     for c in range(total):
         part = doppler[c * outer:(c + 1) * outer]
         value = complex_mul((part[:, :LANES], part[:, LANES:]), turn)
         rows.append(jnp.concatenate(value, axis=1).astype(BF16))
     stacked = jnp.concatenate(rows, axis=0)
-    image = dot_f32(stacked, back_ref[0], left) + dot_f32(stacked, back_ref[1], left)
+    image = dot_f32(stacked, back_ref[...], left)
     for c in range(0, total, 2):
         values = []
         for d in range(2):
@@ -354,7 +368,8 @@
     twist = np.stack(unit_roots(outer, LANES, outer * LANES, -1.0)).astype(np.float32)
     square = (2 * LANES, 2 * LANES)
     side = (2 * outer, 2 * outer)
-    return pair(first, side), pair(fore, square), twist, pair(back, square), pair(last, side)
+    half = lambda table: table.reshape(square).astype(ml_dtypes.bfloat16)
+    return pair(first, side), half(fore), twist, half(back), pair(last, side)
 
 
 def chunk_twist(twist, chunk):
@@ -378,7 +393,7 @@
 def azimuth_stage(early, data, turn, outer, ranges):
     chunks = CHUNKS
     count = data.shape[0]
-    block = 16 // chunks
+    block = 24 // chunks
     first, fore, twist, back, last = azimuth_tables(outer, ranges)
     constants = [jnp.asarray(first), jnp.asarray(fore), chunk_twist(twist, chunks - 1),
                  jnp.asarray(twist), turn, jnp.asarray(back), jnp.asarray(last)]

time: 162 us -> 159 us (0.981)
    pallas_call x1, Pallas kernels: 5.67 us -> 3.61 us  [azimuth_stage(): pl.pallas_call(functools.partial(azimuth_kernel, outer), grid=(count // b...]
where the time goes in v2:
time: 159 us; the launch traced here: 158 us
  waiting for transfers between devices  75 us (47%)
  starting transfers between devices  51.8 us (33%)
  Pallas kernels  14.6 us (9%)
  local copies, waits for them, and re-layouts  7.8 us (5%)
  other arithmetic  6.74 us (4%)
  between operations  2.08 us (1%)
    ppermute x6, waiting for transfers between devices, body(): blocks.append(lax.ppermute(block, 'range', route))  43.7 us
    all_to_all x2, waiting for transfers between devices, body(): lax.all_to_all(blocks, ('range', 'pulse'), split_axis=0, concat_axis=0, t...  21.5 us
    all_to_all x2, starting transfers between devices, body(): lax.all_to_all(blocks, ('range', 'pulse'), split_axis=0, concat_axis=0, t...  21.2 us
    ppermute x6, starting transfers between devices, body(): blocks.append(lax.ppermute(block, 'range', route))  18.7 us
    ppermute x4, starting transfers between devices, shifted(): return lax.ppermute(block, 'band', route)  11.9 us
    ppermute x4, waiting for transfers between devices, shifted(): return lax.ppermute(block, 'band', route)  9.77 us
    pallas_call x2, Pallas kernels, cells_stage(): pl.pallas_call(functools.partial(cells_kernel, outer, sub, sources, first...  4.5 us
    pallas_call x1, Pallas kernels, azimuth_stage(): pl.pallas_call(functools.partial(azimuth_kernel, outer), grid=(count // b...  3.61 us
  transfers between devices with their start and end apart: 12, of which 9 were waited for; matrix products, arithmetic and copies ran while one was open for 6% of the time, Pallas kernels for 4%

profile of v2, /device:TPU:2, one launch (start us, length us, event | category | flops | bytes accessed | tf_op | source)
XLA Modules:
  0.0 158.0 jit_solution(7132705422928209747)
XLA Ops:
  0.0 2.0 %dynamic-slice_bitcast_fusion = (bf16[2,64,1024]{2,1,0:T(8,128)(2,1)S(1)}, bf16[2,64,1024]{2,1,0:T(8,128)(2,1)}, bf16[2,64,1024]{2,1,0:T(8,128)(2,1)}) fusion(bf16[1,2,512,1024]{3,2,1,0:T(8,128)(2,1)} %param.17, s32[]{:T(128)S(6)} %select_n.175, s32[]{:T(128)S(6)} %select_n.173, s32[]{:T(128)S(6)} %select_n.171), kind=kLoop, calls=%fused_computation.3 | loop fusion | bytes 1572876 | tf_op jit(solution)/shard_map/dynamic_slice | solution.py:478
  2.0 6.3 %collective-permute-start = (bf16[2,64,1024]{2,1,0:T(8,128)(2,1)}, bf16[2,64,1024]{2,1,0:T(8,128)(2,1)S(1)}, u32[]{:S(2)}, u32[]{:S(2)}) collective-permute-start(bf16[2,64,1024]{2,1,0:T(8,128)(2,1)} %get-tuple-element.21), channel_id=1, source_target_pairs={{0,3},{1,0},{2,1},{3,2},{4,7},{5,4},{6,5},{7,6},{8,11},{9,8},{10,9... | collective-permute-start | bytes 786440 | tf_op jit(solution)/shard_map/ppermute | solution.py:480
  9.2 2.9 %collective-permute-start.2 = (bf16[2,64,1024]{2,1,0:T(8,128)(2,1)S(1)}, bf16[2,64,1024]{2,1,0:T(8,128)(2,1)S(1)}, u32[]{:S(2)}, u32[]{:S(2)}) collective-permute-start(bf16[2,64,1024]{2,1,0:T(8,128)(2,1)S(1)} %get-tuple-element.19), channel_id=1, source_target_pairs={{0,1},{1,2},{2,3},{3,0},{4,5},{5,6},{6,7},{7,4},{8,9},{9,10},{10,1... | collective-permute-start | bytes 786440 | tf_op jit(solution)/shard_map/ppermute | solution.py:480
  12.1 1.4 fusion.26
  17.3 1.2 fusion.7
  20.0 1.3 pad_add_fusion.scalar_ref
  21.5 9.5 %collective-permute-done.refs_0_ = bf16[2,64,1024]{2,1,0:T(8,128)(2,1)S(1)} collective-permute-done((bf16[2,64,1024]{2,1,0:T(8,128)(2,1)}, bf16[2,64,1024]{2,1,0:T(8,128)(2,1)S(1)}, u32[]{:S(2)}, u32[]{:S(2)}) %collective-permute-start) | collective-permute-done | bytes 262176 | tf_op jit(solution)/shard_map/ppermute | solution.py:480
  31.1 2.3 %cells_stage.2 = (bf16[2,16,128,256]{3,2,1,0:T(8,128)(2,1)S(1)}, bf16[1024,128]{1,0:T(8,128)(2,1)S(1)}) custom-call(s32[4]{0:T(128)S(1)} %pad_add_fusion.scalar_ref, bf16[2,4,2,64,1024]{4,3,2,1,0:T(8,128)(2,1)S(1)} %bitcast.42, bf16[2,64,1024]{2,1,0:T(8,128)(2,1)S(1)} %collective-permute-done.refs_0_, ...), custom_call_target="tpu_custom_call" | custom-call | tf_op jit(solution)/shard_map/cells_stage/pallas_call | solution.py:208
  33.3 3.4 %collective-permute-start.3 = (bf16[1024,128]{1,0:T(8,128)(2,1)S(1)}, bf16[1024,128]{1,0:T(8,128)(2,1)S(1)}, u32[]{:S(2)}, u32[]{:S(2)}) collective-permute-start(bf16[1024,128]{1,0:T(8,128)(2,1)S(1)} %get-tuple-element.10), channel_id=1, source_target_pairs={{0,64},{64,128},{128,192},{1,65},{65,129},{129,193},{2,66},{66,130... | collective-permute-start | bytes 786440 | tf_op jit(solution)/shard_map/ppermute | solution.py:419
  36.7 2.5 %collective-permute-start.4 = (bf16[1024,128]{1,0:T(8,128)(2,1)S(1)}, bf16[1024,128]{1,0:T(8,128)(2,1)S(1)}, u32[]{:S(2)}, u32[]{:S(2)}) collective-permute-start(bf16[1024,128]{1,0:T(8,128)(2,1)S(1)} %get-tuple-element.10), channel_id=1, source_target_pairs={{64,0},{128,64},{192,128},{65,1},{129,65},{193,129},{66,2},{130,66... | collective-permute-start | bytes 786440 | tf_op jit(solution)/shard_map/ppermute | solution.py:419
  39.2 1.2 owned_stage.2.own_ref
  41.6 3.4 %collective-permute-done.4.high_ref = bf16[1024,128]{1,0:T(8,128)(2,1)S(1)} collective-permute-done((bf16[1024,128]{1,0:T(8,128)(2,1)S(1)}, bf16[1024,128]{1,0:T(8,128)(2,1)S(1)}, u32[]{:S(2)}, u32[]{:S(2)}) %collective-permute-start.4) | collective-permute-done | bytes 262176 | tf_op jit(solution)/shard_map/ppermute | solution.py:419
  45.0 1.7 %stitch.2.refs_8_ = bf16[4,16,48,128]{3,2,1,0:T(8,128)(2,1)} custom-call(s32[4]{0:T(128)S(1)} %pad_add_fusion.scalar_ref, bf16[3072,128]{1,0:T(8,128)(2,1)S(1)} %owned_stage.2.own_ref, bf16[1024,128]{1,0:T(8,128)(2,1)S(1)} %collective-permute-done.3.low_ref, bf16[1024,128]{1,0:T(8,128)(2,1)S(1)} %collective-permute-done.4.high_ref), custom_call_target="tpu_custom_call" | custom-call | tf_op jit(solution)/shard_map/stitch/pallas_call | solution.py:279
  46.7 13.9 %all-to-all-start = ((bf16[64,24,2,128]{3,2,1,0:T(2,128)(2,1)}), bf16[64,24,2,128]{3,2,1,0:T(2,128)(2,1)S(1)}, u32[]{:S(2)}, u32[]{:S(2)}) async-start(bf16[64,24,2,128]{3,2,1,0:T(2,128)(2,1)} %bitcast.21), calls=%async_computation | async-start | bytes 1572864 | tf_op jit(solution)/shard_map/all_to_all | solution.py:504
  60.6 1.2 constant_dynamic-slice_fusion
  61.8 4.0 %collective-permute-start.5 = (bf16[2,64,1024]{2,1,0:T(8,128)(2,1)S(1)}, bf16[2,64,1024]{2,1,0:T(8,128)(2,1)S(1)}, u32[]{:S(2)}, u32[]{:S(2)}) collective-permute-start(bf16[2,64,1024]{2,1,0:T(8,128)(2,1)S(1)} %get-tuple-element.18), channel_id=1, source_target_pairs={{0,3},{1,0},{2,1},{3,2},{4,7},{5,4},{6,5},{7,6},{8,11},{9,8},{10,9... | collective-permute-start | bytes 786440 | tf_op jit(solution)/shard_map/ppermute | solution.py:480
  65.8 2.2 %collective-permute-start.6 = (bf16[2,64,1024]{2,1,0:T(8,128)(2,1)S(1)}, bf16[2,64,1024]{2,1,0:T(8,128)(2,1)S(1)}, u32[]{:S(2)}, u32[]{:S(2)}) collective-permute-start(bf16[2,64,1024]{2,1,0:T(8,128)(2,1)S(1)} %get-tuple-element.17), channel_id=1, source_target_pairs={{0,2},{1,3},{2,0},{3,1},{4,6},{5,7},{6,4},{7,5},{8,10},{9,11},{10,... | collective-permute-start | bytes 786440 | tf_op jit(solution)/shard_map/ppermute | solution.py:480
  67.9 2.5 %collective-permute-start.7 = (bf16[2,64,1024]{2,1,0:T(8,128)(2,1)S(1)}, bf16[2,64,1024]{2,1,0:T(8,128)(2,1)S(1)}, u32[]{:S(2)}, u32[]{:S(2)}) collective-permute-start(bf16[2,64,1024]{2,1,0:T(8,128)(2,1)S(1)} %get-tuple-element.16), channel_id=1, source_target_pairs={{0,1},{1,2},{2,3},{3,0},{4,5},{5,6},{6,7},{7,4},{8,9},{9,10},{10,1... | collective-permute-start | bytes 786440 | tf_op jit(solution)/shard_map/ppermute | solution.py:480
  70.4 22.9 %collective-permute-done.5.refs_0_ = bf16[2,64,1024]{2,1,0:T(8,128)(2,1)S(1)} collective-permute-done((bf16[2,64,1024]{2,1,0:T(8,128)(2,1)S(1)}, bf16[2,64,1024]{2,1,0:T(8,128)(2,1)S(1)}, u32[]{:S(2)}, u32[]{:S(2)}) %collective-permute-start.5) | collective-permute-done | bytes 262176 | tf_op jit(solution)/shard_map/ppermute | solution.py:480
  93.3 7.6 %collective-permute-done.6.refs_1_ = bf16[2,64,1024]{2,1,0:T(8,128)(2,1)S(1)} collective-permute-done((bf16[2,64,1024]{2,1,0:T(8,128)(2,1)S(1)}, bf16[2,64,1024]{2,1,0:T(8,128)(2,1)S(1)}, u32[]{:S(2)}, u32[]{:S(2)}) %collective-permute-start.6) | collective-permute-done | bytes 262176 | tf_op jit(solution)/shard_map/ppermute | solution.py:480
  100.9 3.7 %collective-permute-done.7.refs_2_ = bf16[2,64,1024]{2,1,0:T(8,128)(2,1)S(1)} collective-permute-done((bf16[2,64,1024]{2,1,0:T(8,128)(2,1)S(1)}, bf16[2,64,1024]{2,1,0:T(8,128)(2,1)S(1)}, u32[]{:S(2)}, u32[]{:S(2)}) %collective-permute-start.7) | collective-permute-done | bytes 262176 | tf_op jit(solution)/shard_map/ppermute | solution.py:480
  104.6 1.6 %copy-done.1 = bf16[1,2,512,1024]{3,2,1,0:T(8,128)(2,1)S(1)} copy-done((bf16[1,2,512,1024]{3,2,1,0:T(8,128)(2,1)S(1)}, bf16[1,2,512,1024]{3,2,1,0:T(8,128)(2,1)}, u32[]{:S(2)}) %copy-start.1) | copy-done | bytes 2097176
  106.2 2.2 %cells_stage.3 = (bf16[2,16,128,256]{3,2,1,0:T(8,128)(2,1)S(1)}, bf16[1024,128]{1,0:T(8,128)(2,1)S(1)}) custom-call(s32[4]{0:T(128)S(1)} %pad_add_fusion.scalar_ref, bf16[2,4,2,64,1024]{4,3,2,1,0:T(8,128)(2,1)S(1)} %bitcast.43, bf16[2,64,1024]{2,1,0:T(8,128)(2,1)S(1)} %collective-permute-done.5.refs_0_, ...), custom_call_target="tpu_custom_call" | custom-call | tf_op jit(solution)/shard_map/cells_stage/pallas_call | solution.py:208
  108.4 3.1 %collective-permute-start.8 = (bf16[1024,128]{1,0:T(8,128)(2,1)S(1)}, bf16[1024,128]{1,0:T(8,128)(2,1)S(1)}, u32[]{:S(2)}, u32[]{:S(2)}) collective-permute-start(bf16[1024,128]{1,0:T(8,128)(2,1)S(1)} %get-tuple-element.12), channel_id=1, source_target_pairs={{0,64},{64,128},{128,192},{1,65},{65,129},{129,193},{2,66},{66,130... | collective-permute-start | bytes 786440 | tf_op jit(solution)/shard_map/ppermute | solution.py:419
  111.5 2.9 %collective-permute-start.9 = (bf16[1024,128]{1,0:T(8,128)(2,1)S(1)}, bf16[1024,128]{1,0:T(8,128)(2,1)S(1)}, u32[]{:S(2)}, u32[]{:S(2)}) collective-permute-start(bf16[1024,128]{1,0:T(8,128)(2,1)S(1)} %get-tuple-element.12), channel_id=1, source_target_pairs={{64,0},{128,64},{192,128},{65,1},{129,65},{193,129},{66,2},{130,66... | collective-permute-start | bytes 786440 | tf_op jit(solution)/shard_map/ppermute | solution.py:419
  114.5 1.2 owned_stage.3.own_ref
  115.7 2.4 %collective-permute-done.8.low_ref = bf16[1024,128]{1,0:T(8,128)(2,1)S(1)} collective-permute-done((bf16[1024,128]{1,0:T(8,128)(2,1)S(1)}, bf16[1024,128]{1,0:T(8,128)(2,1)S(1)}, u32[]{:S(2)}, u32[]{:S(2)}) %collective-permute-start.8) | collective-permute-done | bytes 262176 | tf_op jit(solution)/shard_map/ppermute | solution.py:419
  118.1 2.8 %collective-permute-done.9.high_ref = bf16[1024,128]{1,0:T(8,128)(2,1)S(1)} collective-permute-done((bf16[1024,128]{1,0:T(8,128)(2,1)S(1)}, bf16[1024,128]{1,0:T(8,128)(2,1)S(1)}, u32[]{:S(2)}, u32[]{:S(2)}) %collective-permute-start.9) | collective-permute-done | bytes 262176 | tf_op jit(solution)/shard_map/ppermute | solution.py:419
  120.9 1.7 %stitch.3 = bf16[4,16,48,128]{3,2,1,0:T(8,128)(2,1)} custom-call(s32[4]{0:T(128)S(1)} %pad_add_fusion.scalar_ref, bf16[3072,128]{1,0:T(8,128)(2,1)S(1)} %owned_stage.3.own_ref, bf16[1024,128]{1,0:T(8,128)(2,1)S(1)} %collective-permute-done.8.low_ref, bf16[1024,128]{1,0:T(8,128)(2,1)S(1)} %collective-permute-done.9.high_ref), custom_call_target="tpu_custom_call" | custom-call | tf_op jit(solution)/shard_map/stitch/pallas_call | solution.py:279
  122.6 7.4 %all-to-all-start.1 = ((bf16[64,24,2,128]{3,2,1,0:T(2,128)(2,1)}), bf16[64,24,2,128]{3,2,1,0:T(2,128)(2,1)S(1)}, u32[]{:S(2)}, u32[]{:S(2)}) async-start(bf16[64,24,2,128]{3,2,1,0:T(2,128)(2,1)} %bitcast.26), calls=%async_computation.1 | async-start | bytes 1572864 | tf_op jit(solution)/shard_map/all_to_all | solution.py:504
  132.0 21.5 %all-to-all-done.1 = bf16[64,24,2,128]{3,2,1,0:T(2,128)(2,1)S(1)} async-done(((bf16[64,24,2,128]{3,2,1,0:T(2,128)(2,1)}), bf16[64,24,2,128]{3,2,1,0:T(2,128)(2,1)S(1)}, u32[]{:S(2)}, u32[]{:S(2)}) %all-to-all-start.1) | async-done | bytes 786464 | tf_op jit(solution)/shard_map/all_to_all | solution.py:504
  154.4 3.6 %azimuth_stage.1 = bf16[48,128,128]{2,1,0:T(8,128)(2,1)} custom-call(bf16[2,128,128]{2,1,0:T(8,128)(2,1)S(1)} %copy-done.4, bf16[256,256]{1,0:T(8,128)(2,1)S(1)} %copy-done.5, f32[2,64,128]{2,1,0:T(8,128)S(1)} %copy-done.7, f32[2,64,128]{2,1,0:T(8,128)S(1)} %copy-done.8, f32[2,64,128]{2,1,0:T(8,128)S(1)} %pad_maximum_fusion.3.filter_ref, ...), custom_call_target="tpu_custom_call" | custom-call | tf_op jit(solution)/shard_map/azimuth_stage/pallas_call | solution.py:403
  (65 shorter events, 8.6 us)
Async XLA Ops:
  2.0 29.1 %collective-permute-start = (bf16[2,64,1024]{2,1,0:T(8,128)(2,1)}, bf16[2,64,1024]{2,1,0:T(8,128)(2,1)S(1)}, u32[]{:S(2)}, u32[]{:S(2)}) collective-permute-start(bf16[2,64,1024]{2,1,0:T(8,128)(2,1)} %get-tuple-element.21), channel_id=1, source_target_pairs={{0,3},{1,0},{2,1},{3,2},{4,7},{5,4},{6,5},{7,6},{8,11},{9,8},{10,9... | collective-permute-start | bytes 786440 | tf_op jit(solution)/shard_map/ppermute | solution.py:480
  8.3 22.8 %collective-permute-start.1 = (bf16[2,64,1024]{2,1,0:T(8,128)(2,1)}, bf16[2,64,1024]{2,1,0:T(8,128)(2,1)S(1)}, u32[]{:S(2)}, u32[]{:S(2)}) collective-permute-start(bf16[2,64,1024]{2,1,0:T(8,128)(2,1)} %get-tuple-element.20), channel_id=1, source_target_pairs={{0,2},{1,3},{2,0},{3,1},{4,6},{5,7},{6,4},{7,5},{8,10},{9,11},{10,... | collective-permute-start | bytes 786440 | tf_op jit(solution)/shard_map/ppermute | solution.py:480
  9.2 21.9 %collective-permute-start.2 = (bf16[2,64,1024]{2,1,0:T(8,128)(2,1)S(1)}, bf16[2,64,1024]{2,1,0:T(8,128)(2,1)S(1)}, u32[]{:S(2)}, u32[]{:S(2)}) collective-permute-start(bf16[2,64,1024]{2,1,0:T(8,128)(2,1)S(1)} %get-tuple-element.19), channel_id=1, source_target_pairs={{0,1},{1,2},{2,3},{3,0},{4,5},{5,6},{6,7},{7,4},{8,9},{9,10},{10,1... | collective-permute-start | bytes 786440 | tf_op jit(solution)/shard_map/ppermute | solution.py:480
  21.3 9.7 %copy-start = (bf16[1,2,512,1024]{3,2,1,0:T(8,128)(2,1)S(1)}, bf16[1,2,512,1024]{3,2,1,0:T(8,128)(2,1)}, u32[]{:S(2)}) copy-start(bf16[1,2,512,1024]{3,2,1,0:T(8,128)(2,1)} %param.17) | copy-start | bytes 6291460
  21.3 9.7 %copy-start.3 = (bf16[128,256]{1,0:T(8,128)(2,1)S(1)}, bf16[128,256]{1,0:T(8,128)(2,1)}, u32[]{:S(2)}) copy-start(bf16[128,256]{1,0:T(8,128)(2,1)} %constant.149.clone.refs_7_) | copy-start | bytes 196612
  31.1 8.1 %copy-start.2 = (bf16[384,256]{1,0:T(8,128)(2,1)S(1)}, bf16[384,256]{1,0:T(8,128)(2,1)}, u32[]{:S(2)}) copy-start(bf16[384,256]{1,0:T(8,128)(2,1)} %constant.150.clone.table_ref) | copy-start | bytes 589828
  33.3 8.3 %collective-permute-start.3 = (bf16[1024,128]{1,0:T(8,128)(2,1)S(1)}, bf16[1024,128]{1,0:T(8,128)(2,1)S(1)}, u32[]{:S(2)}, u32[]{:S(2)}) collective-permute-start(bf16[1024,128]{1,0:T(8,128)(2,1)S(1)} %get-tuple-element.10), channel_id=1, source_target_pairs={{0,64},{64,128},{128,192},{1,65},{65,129},{129,193},{2,66},{66,130... | collective-permute-start | bytes 786440 | tf_op jit(solution)/shard_map/ppermute | solution.py:419
  36.7 8.3 %collective-permute-start.4 = (bf16[1024,128]{1,0:T(8,128)(2,1)S(1)}, bf16[1024,128]{1,0:T(8,128)(2,1)S(1)}, u32[]{:S(2)}, u32[]{:S(2)}) collective-permute-start(bf16[1024,128]{1,0:T(8,128)(2,1)S(1)} %get-tuple-element.10), channel_id=1, source_target_pairs={{64,0},{128,64},{192,128},{65,1},{129,65},{193,129},{66,2},{130,66... | collective-permute-start | bytes 786440 | tf_op jit(solution)/shard_map/ppermute | solution.py:419
  46.7 23.7 %copy-start.11 = (f32[1,128,128]{2,1,0:T(8,128)S(1)}, f32[1,128,128]{2,1,0:T(8,128)}, u32[]{:S(2)}) copy-start(f32[1,128,128]{2,1,0:T(8,128)} %get-tuple-element.35) | copy-start | bytes 196612
  46.7 76.0 %all-to-all-start = ((bf16[64,24,2,128]{3,2,1,0:T(2,128)(2,1)}), bf16[64,24,2,128]{3,2,1,0:T(2,128)(2,1)S(1)}, u32[]{:S(2)}, u32[]{:S(2)}) async-start(bf16[64,24,2,128]{3,2,1,0:T(2,128)(2,1)} %bitcast.21), calls=%async_computation | async-start | bytes 1572864 | tf_op jit(solution)/shard_map/all_to_all | solution.py:504
  61.8 31.5 %collective-permute-start.5 = (bf16[2,64,1024]{2,1,0:T(8,128)(2,1)S(1)}, bf16[2,64,1024]{2,1,0:T(8,128)(2,1)S(1)}, u32[]{:S(2)}, u32[]{:S(2)}) collective-permute-start(bf16[2,64,1024]{2,1,0:T(8,128)(2,1)S(1)} %get-tuple-element.18), channel_id=1, source_target_pairs={{0,3},{1,0},{2,1},{3,2},{4,7},{5,4},{6,5},{7,6},{8,11},{9,8},{10,9... | collective-permute-start | bytes 786440 | tf_op jit(solution)/shard_map/ppermute | solution.py:480
  65.8 35.1 %collective-permute-start.6 = (bf16[2,64,1024]{2,1,0:T(8,128)(2,1)S(1)}, bf16[2,64,1024]{2,1,0:T(8,128)(2,1)S(1)}, u32[]{:S(2)}, u32[]{:S(2)}) collective-permute-start(bf16[2,64,1024]{2,1,0:T(8,128)(2,1)S(1)} %get-tuple-element.17), channel_id=1, source_target_pairs={{0,2},{1,3},{2,0},{3,1},{4,6},{5,7},{6,4},{7,5},{8,10},{9,11},{10,... | collective-permute-start | bytes 786440 | tf_op jit(solution)/shard_map/ppermute | solution.py:480
  67.9 36.7 %collective-permute-start.7 = (bf16[2,64,1024]{2,1,0:T(8,128)(2,1)S(1)}, bf16[2,64,1024]{2,1,0:T(8,128)(2,1)S(1)}, u32[]{:S(2)}, u32[]{:S(2)}) collective-permute-start(bf16[2,64,1024]{2,1,0:T(8,128)(2,1)S(1)} %get-tuple-element.16), channel_id=1, source_target_pairs={{0,1},{1,2},{2,3},{3,0},{4,5},{5,6},{6,7},{7,4},{8,9},{9,10},{10,1... | collective-permute-start | bytes 786440 | tf_op jit(solution)/shard_map/ppermute | solution.py:480
  104.6 1.6 %copy-start.1 = (bf16[1,2,512,1024]{3,2,1,0:T(8,128)(2,1)S(1)}, bf16[1,2,512,1024]{3,2,1,0:T(8,128)(2,1)}, u32[]{:S(2)}) copy-start(bf16[1,2,512,1024]{3,2,1,0:T(8,128)(2,1)} %param.17) | copy-start | bytes 6291460
  108.4 9.7 %collective-permute-start.8 = (bf16[1024,128]{1,0:T(8,128)(2,1)S(1)}, bf16[1024,128]{1,0:T(8,128)(2,1)S(1)}, u32[]{:S(2)}, u32[]{:S(2)}) collective-permute-start(bf16[1024,128]{1,0:T(8,128)(2,1)S(1)} %get-tuple-element.12), channel_id=1, source_target_pairs={{0,64},{64,128},{128,192},{1,65},{65,129},{129,193},{2,66},{66,130... | collective-permute-start | bytes 786440 | tf_op jit(solution)/shard_map/ppermute | solution.py:419
  111.5 9.4 %collective-permute-start.9 = (bf16[1024,128]{1,0:T(8,128)(2,1)S(1)}, bf16[1024,128]{1,0:T(8,128)(2,1)S(1)}, u32[]{:S(2)}, u32[]{:S(2)}) collective-permute-start(bf16[1024,128]{1,0:T(8,128)(2,1)S(1)} %get-tuple-element.12), channel_id=1, source_target_pairs={{64,0},{128,64},{192,128},{65,1},{129,65},{193,129},{66,2},{130,66... | collective-permute-start | bytes 786440 | tf_op jit(solution)/shard_map/ppermute | solution.py:419
  115.7 14.3 %copy-start.12 = (f32[8192]{0:T(1024)S(1)}, f32[8192]{0:T(1024)}, u32[]{:S(2)}) copy-start(f32[8192]{0:T(1024)} %param.21) | copy-start | bytes 98308
  122.6 8.7 %copy-start.4 = (bf16[2,128,128]{2,1,0:T(8,128)(2,1)S(1)}, bf16[2,128,128]{2,1,0:T(8,128)(2,1)}, u32[]{:S(2)}) copy-start(bf16[2,128,128]{2,1,0:T(8,128)(2,1)} %constant.151.clone.first_ref) | copy-start | bytes 196612
  122.6 8.7 %copy-start.10 = (f32[2,64,128]{2,1,0:T(8,128)S(1)}, f32[2,64,128]{2,1,0:T(8,128)}, u32[]{:S(2)}) copy-start(f32[2,64,128]{2,1,0:T(8,128)} %constant.152.clone.twist_ref) | copy-start | bytes 196612
  122.6 30.9 %all-to-all-start.1 = ((bf16[64,24,2,128]{3,2,1,0:T(2,128)(2,1)}), bf16[64,24,2,128]{3,2,1,0:T(2,128)(2,1)S(1)}, u32[]{:S(2)}, u32[]{:S(2)}) async-start(bf16[64,24,2,128]{3,2,1,0:T(2,128)(2,1)} %bitcast.26), calls=%async_computation.1 | async-start | bytes 1572864 | tf_op jit(solution)/shard_map/all_to_all | solution.py:504
  130.5 23.9 %copy-start.5 = (bf16[256,256]{1,0:T(8,128)(2,1)S(1)}, bf16[256,256]{1,0:T(8,128)(2,1)}, u32[]{:S(2)}) copy-start(bf16[256,256]{1,0:T(8,128)(2,1)} %constant.153.clone.fore_ref) | copy-start | bytes 393220
  130.5 23.8 %copy-start.6 = (bf16[256,256]{1,0:T(8,128)(2,1)S(1)}, bf16[256,256]{1,0:T(8,128)(2,1)}, u32[]{:S(2)}) copy-start(bf16[256,256]{1,0:T(8,128)(2,1)} %constant.156.clone.back_ref) | copy-start | bytes 393220
  130.5 23.8 %copy-start.7 = (f32[2,64,128]{2,1,0:T(8,128)S(1)}, f32[2,64,128]{2,1,0:T(8,128)}, u32[]{:S(2)}) copy-start(f32[2,64,128]{2,1,0:T(8,128)} %constant.154.clone.twist_ref) | copy-start | bytes 196612
  130.5 23.8 %copy-start.8 = (f32[2,64,128]{2,1,0:T(8,128)S(1)}, f32[2,64,128]{2,1,0:T(8,128)}, u32[]{:S(2)}) copy-start(f32[2,64,128]{2,1,0:T(8,128)} %constant.155.clone.back_twist_ref) | copy-start | bytes 196612
  130.5 23.8 %copy-start.9 = (bf16[2,128,128]{2,1,0:T(8,128)(2,1)S(1)}, bf16[2,128,128]{2,1,0:T(8,128)(2,1)}, u32[]{:S(2)}) copy-start(bf16[2,128,128]{2,1,0:T(8,128)(2,1)} %constant.157.clone.last_ref) | copy-start | bytes 196612

commit v3 on v2

--- a/solution.py
+++ b/solution.py
@@ -291,7 +291,7 @@
 def spread_rows(first_ref, data, twist_ref):
     left = ((1,), (0,))
     wide = jnp.concatenate(data, axis=1)
-    spread = dot_f32(first_ref[0], wide, left) + dot_f32(first_ref[1], wide, left)
+    spread = dot_f32(first_ref[...], wide, left)
     half = spread.shape[0] // 2
     twist = (twist_ref[0], twist_ref[1])
     rows = []
@@ -319,7 +319,6 @@
     twist_back = (back_twist_ref[0], -back_twist_ref[1])
     turn = (filter_ref[0], filter_ref[1])
     left = ((1,), (0,))
-    two = lambda lhs, rhs: dot_f32(lhs[0], rhs, left) + dot_f32(lhs[1], rhs, left)
     rows = []
     for c in range(0, data_ref.shape[0], 2):
         rows += spread_rows(first_ref, (data_ref[c], data_ref[c + 1]), twist_ref)
@@ -341,7 +340,7 @@
             part = image[(c + d) * outer:(c + d + 1) * outer]
             value = complex_mul((part[:, :LANES], part[:, LANES:]), twist_back)
             values.append(jnp.concatenate(value, axis=0).astype(BF16))
-        value = two((last_ref[0], last_ref[1]), jnp.concatenate(values, axis=1)).astype(BF16)
+        value = dot_f32(last_ref[...], jnp.concatenate(values, axis=1), left).astype(BF16)
         out_ref[c] = value[:, :LANES]
         out_ref[c + 1] = value[:, LANES:]
 
@@ -363,13 +362,12 @@
     back = np.zeros((2, LANES, 2, LANES))
     back[0, :, 0], back[0, :, 1] = cos, -sin
     back[1, :, 0], back[1, :, 1] = sin, cos
-    pair = lambda table, shape: np.stack(split_const(table.reshape(shape)))
+    half = lambda table, shape: table.reshape(shape).astype(ml_dtypes.bfloat16)
     fore = fore.reshape(2, CHUNKS, LANES // CHUNKS, 2 * LANES).transpose(1, 0, 2, 3)
     twist = np.stack(unit_roots(outer, LANES, outer * LANES, -1.0)).astype(np.float32)
     square = (2 * LANES, 2 * LANES)
     side = (2 * outer, 2 * outer)
-    half = lambda table: table.reshape(square).astype(ml_dtypes.bfloat16)
-    return pair(first, side), half(fore), twist, half(back), pair(last, side)
+    return half(first, side), half(fore, square), twist, half(back, square), half(last, side)
 
 
 def chunk_twist(twist, chunk):

time: 159 us -> 158 us (level)
  no operation moved by 1% of the time
where the time goes in v3:
time: 158 us
  waiting for transfers between devices  75.1 us (48%)
  starting transfers between devices  51.8 us (33%)
  Pallas kernels  14 us (9%)
  local copies, waits for them, and re-layouts  7.8 us (5%)
  other arithmetic  6.74 us (4%)
  between operations  2.08 us (1%)
    ppermute x6, waiting for transfers between devices, body(): blocks.append(lax.ppermute(block, 'range', route))  43.7 us
    all_to_all x2, waiting for transfers between devices, body(): lax.all_to_all(blocks, ('range', 'pulse'), split_axis=0, concat_axis=0, t...  21.7 us
    all_to_all x2, starting transfers between devices, body(): lax.all_to_all(blocks, ('range', 'pulse'), split_axis=0, concat_axis=0, t...  21.2 us
    ppermute x6, starting transfers between devices, body(): blocks.append(lax.ppermute(block, 'range', route))  18.7 us
    ppermute x4, starting transfers between devices, shifted(): return lax.ppermute(block, 'band', route)  11.9 us
    ppermute x4, waiting for transfers between devices, shifted(): return lax.ppermute(block, 'band', route)  9.77 us
    pallas_call x2, Pallas kernels, cells_stage(): pl.pallas_call(functools.partial(cells_kernel, outer, sub, sources, first...  4.5 us
    pallas_call x2, Pallas kernels, stitch(): pl.pallas_call(functools.partial(stitch_kernel, sub), in_specs=[pl.BlockS...  3.33 us
  transfers between devices with their start and end apart: 12, of which 9 were waited for; matrix products, arithmetic and copies ran while one was open for 6% of the time, Pallas kernels for 4%

profile of v3, /device:TPU:2, one launch (start us, length us, event | category | flops | bytes accessed | tf_op | source)
XLA Modules:
  0.0 157.5 jit_solution(159965733869086304)
XLA Ops:
  0.0 2.0 %dynamic-slice_bitcast_fusion = (bf16[2,64,1024]{2,1,0:T(8,128)(2,1)S(1)}, bf16[2,64,1024]{2,1,0:T(8,128)(2,1)}, bf16[2,64,1024]{2,1,0:T(8,128)(2,1)}) fusion(bf16[1,2,512,1024]{3,2,1,0:T(8,128)(2,1)} %param.17, s32[]{:T(128)S(6)} %select_n.175, s32[]{:T(128)S(6)} %select_n.173, s32[]{:T(128)S(6)} %select_n.171), kind=kLoop, calls=%fused_computation.3 | loop fusion | bytes 1572876 | tf_op jit(solution)/shard_map/dynamic_slice | solution.py:476
  2.0 6.3 %collective-permute-start = (bf16[2,64,1024]{2,1,0:T(8,128)(2,1)}, bf16[2,64,1024]{2,1,0:T(8,128)(2,1)S(1)}, u32[]{:S(2)}, u32[]{:S(2)}) collective-permute-start(bf16[2,64,1024]{2,1,0:T(8,128)(2,1)} %get-tuple-element.21), channel_id=1, source_target_pairs={{0,3},{1,0},{2,1},{3,2},{4,7},{5,4},{6,5},{7,6},{8,11},{9,8},{10,9... | collective-permute-start | bytes 786440 | tf_op jit(solution)/shard_map/ppermute | solution.py:478
  9.2 2.9 %collective-permute-start.2 = (bf16[2,64,1024]{2,1,0:T(8,128)(2,1)S(1)}, bf16[2,64,1024]{2,1,0:T(8,128)(2,1)S(1)}, u32[]{:S(2)}, u32[]{:S(2)}) collective-permute-start(bf16[2,64,1024]{2,1,0:T(8,128)(2,1)S(1)} %get-tuple-element.19), channel_id=1, source_target_pairs={{0,1},{1,2},{2,3},{3,0},{4,5},{5,6},{6,7},{7,4},{8,9},{9,10},{10,1... | collective-permute-start | bytes 786440 | tf_op jit(solution)/shard_map/ppermute | solution.py:478
  12.1 1.4 fusion.26
  17.3 1.2 fusion.7
  20.0 1.3 pad_add_fusion.scalar_ref
  21.5 9.5 %collective-permute-done.refs_0_ = bf16[2,64,1024]{2,1,0:T(8,128)(2,1)S(1)} collective-permute-done((bf16[2,64,1024]{2,1,0:T(8,128)(2,1)}, bf16[2,64,1024]{2,1,0:T(8,128)(2,1)S(1)}, u32[]{:S(2)}, u32[]{:S(2)}) %collective-permute-start) | collective-permute-done | bytes 262176 | tf_op jit(solution)/shard_map/ppermute | solution.py:478
  31.1 2.3 %cells_stage.2 = (bf16[2,16,128,256]{3,2,1,0:T(8,128)(2,1)S(1)}, bf16[1024,128]{1,0:T(8,128)(2,1)S(1)}) custom-call(s32[4]{0:T(128)S(1)} %pad_add_fusion.scalar_ref, bf16[2,4,2,64,1024]{4,3,2,1,0:T(8,128)(2,1)S(1)} %bitcast.42, bf16[2,64,1024]{2,1,0:T(8,128)(2,1)S(1)} %collective-permute-done.refs_0_, ...), custom_call_target="tpu_custom_call" | custom-call | tf_op jit(solution)/shard_map/cells_stage/pallas_call | solution.py:208
  33.3 3.4 %collective-permute-start.3 = (bf16[1024,128]{1,0:T(8,128)(2,1)S(1)}, bf16[1024,128]{1,0:T(8,128)(2,1)S(1)}, u32[]{:S(2)}, u32[]{:S(2)}) collective-permute-start(bf16[1024,128]{1,0:T(8,128)(2,1)S(1)} %get-tuple-element.10), channel_id=1, source_target_pairs={{0,64},{64,128},{128,192},{1,65},{65,129},{129,193},{2,66},{66,130... | collective-permute-start | bytes 786440 | tf_op jit(solution)/shard_map/ppermute | solution.py:417
  36.7 2.5 %collective-permute-start.4 = (bf16[1024,128]{1,0:T(8,128)(2,1)S(1)}, bf16[1024,128]{1,0:T(8,128)(2,1)S(1)}, u32[]{:S(2)}, u32[]{:S(2)}) collective-permute-start(bf16[1024,128]{1,0:T(8,128)(2,1)S(1)} %get-tuple-element.10), channel_id=1, source_target_pairs={{64,0},{128,64},{192,128},{65,1},{129,65},{193,129},{66,2},{130,66... | collective-permute-start | bytes 786440 | tf_op jit(solution)/shard_map/ppermute | solution.py:417
  39.2 1.2 owned_stage.2.own_ref
  41.6 3.4 %collective-permute-done.4.high_ref = bf16[1024,128]{1,0:T(8,128)(2,1)S(1)} collective-permute-done((bf16[1024,128]{1,0:T(8,128)(2,1)S(1)}, bf16[1024,128]{1,0:T(8,128)(2,1)S(1)}, u32[]{:S(2)}, u32[]{:S(2)}) %collective-permute-start.4) | collective-permute-done | bytes 262176 | tf_op jit(solution)/shard_map/ppermute | solution.py:417
  45.0 1.7 %stitch.2.refs_8_ = bf16[4,16,48,128]{3,2,1,0:T(8,128)(2,1)} custom-call(s32[4]{0:T(128)S(1)} %pad_add_fusion.scalar_ref, bf16[3072,128]{1,0:T(8,128)(2,1)S(1)} %owned_stage.2.own_ref, bf16[1024,128]{1,0:T(8,128)(2,1)S(1)} %collective-permute-done.3.low_ref, bf16[1024,128]{1,0:T(8,128)(2,1)S(1)} %collective-permute-done.4.high_ref), custom_call_target="tpu_custom_call" | custom-call | tf_op jit(solution)/shard_map/stitch/pallas_call | solution.py:279
  46.7 13.9 %all-to-all-start = ((bf16[64,24,2,128]{3,2,1,0:T(2,128)(2,1)}), bf16[64,24,2,128]{3,2,1,0:T(2,128)(2,1)S(1)}, u32[]{:S(2)}, u32[]{:S(2)}) async-start(bf16[64,24,2,128]{3,2,1,0:T(2,128)(2,1)} %bitcast.21), calls=%async_computation | async-start | bytes 1572864 | tf_op jit(solution)/shard_map/all_to_all | solution.py:502
  60.6 1.2 constant_dynamic-slice_fusion
  61.8 4.0 %collective-permute-start.5 = (bf16[2,64,1024]{2,1,0:T(8,128)(2,1)S(1)}, bf16[2,64,1024]{2,1,0:T(8,128)(2,1)S(1)}, u32[]{:S(2)}, u32[]{:S(2)}) collective-permute-start(bf16[2,64,1024]{2,1,0:T(8,128)(2,1)S(1)} %get-tuple-element.18), channel_id=1, source_target_pairs={{0,3},{1,0},{2,1},{3,2},{4,7},{5,4},{6,5},{7,6},{8,11},{9,8},{10,9... | collective-permute-start | bytes 786440 | tf_op jit(solution)/shard_map/ppermute | solution.py:478
  65.8 2.2 %collective-permute-start.6 = (bf16[2,64,1024]{2,1,0:T(8,128)(2,1)S(1)}, bf16[2,64,1024]{2,1,0:T(8,128)(2,1)S(1)}, u32[]{:S(2)}, u32[]{:S(2)}) collective-permute-start(bf16[2,64,1024]{2,1,0:T(8,128)(2,1)S(1)} %get-tuple-element.17), channel_id=1, source_target_pairs={{0,2},{1,3},{2,0},{3,1},{4,6},{5,7},{6,4},{7,5},{8,10},{9,11},{10,... | collective-permute-start | bytes 786440 | tf_op jit(solution)/shard_map/ppermute | solution.py:478
  67.9 2.5 %collective-permute-start.7 = (bf16[2,64,1024]{2,1,0:T(8,128)(2,1)S(1)}, bf16[2,64,1024]{2,1,0:T(8,128)(2,1)S(1)}, u32[]{:S(2)}, u32[]{:S(2)}) collective-permute-start(bf16[2,64,1024]{2,1,0:T(8,128)(2,1)S(1)} %get-tuple-element.16), channel_id=1, source_target_pairs={{0,1},{1,2},{2,3},{3,0},{4,5},{5,6},{6,7},{7,4},{8,9},{9,10},{10,1... | collective-permute-start | bytes 786440 | tf_op jit(solution)/shard_map/ppermute | solution.py:478
  70.4 22.9 %collective-permute-done.5.refs_0_ = bf16[2,64,1024]{2,1,0:T(8,128)(2,1)S(1)} collective-permute-done((bf16[2,64,1024]{2,1,0:T(8,128)(2,1)S(1)}, bf16[2,64,1024]{2,1,0:T(8,128)(2,1)S(1)}, u32[]{:S(2)}, u32[]{:S(2)}) %collective-permute-start.5) | collective-permute-done | bytes 262176 | tf_op jit(solution)/shard_map/ppermute | solution.py:478
  93.3 7.6 %collective-permute-done.6.refs_1_ = bf16[2,64,1024]{2,1,0:T(8,128)(2,1)S(1)} collective-permute-done((bf16[2,64,1024]{2,1,0:T(8,128)(2,1)S(1)}, bf16[2,64,1024]{2,1,0:T(8,128)(2,1)S(1)}, u32[]{:S(2)}, u32[]{:S(2)}) %collective-permute-start.6) | collective-permute-done | bytes 262176 | tf_op jit(solution)/shard_map/ppermute | solution.py:478
  100.9 3.7 %collective-permute-done.7.refs_2_ = bf16[2,64,1024]{2,1,0:T(8,128)(2,1)S(1)} collective-permute-done((bf16[2,64,1024]{2,1,0:T(8,128)(2,1)S(1)}, bf16[2,64,1024]{2,1,0:T(8,128)(2,1)S(1)}, u32[]{:S(2)}, u32[]{:S(2)}) %collective-permute-start.7) | collective-permute-done | bytes 262176 | tf_op jit(solution)/shard_map/ppermute | solution.py:478
  104.6 1.6 %copy-done.1 = bf16[1,2,512,1024]{3,2,1,0:T(8,128)(2,1)S(1)} copy-done((bf16[1,2,512,1024]{3,2,1,0:T(8,128)(2,1)S(1)}, bf16[1,2,512,1024]{3,2,1,0:T(8,128)(2,1)}, u32[]{:S(2)}) %copy-start.1) | copy-done | bytes 2097176
  106.2 2.2 %cells_stage.3 = (bf16[2,16,128,256]{3,2,1,0:T(8,128)(2,1)S(1)}, bf16[1024,128]{1,0:T(8,128)(2,1)S(1)}) custom-call(s32[4]{0:T(128)S(1)} %pad_add_fusion.scalar_ref, bf16[2,4,2,64,1024]{4,3,2,1,0:T(8,128)(2,1)S(1)} %bitcast.43, bf16[2,64,1024]{2,1,0:T(8,128)(2,1)S(1)} %collective-permute-done.5.refs_0_, ...), custom_call_target="tpu_custom_call" | custom-call | tf_op jit(solution)/shard_map/cells_stage/pallas_call | solution.py:208
  108.4 3.1 %collective-permute-start.8 = (bf16[1024,128]{1,0:T(8,128)(2,1)S(1)}, bf16[1024,128]{1,0:T(8,128)(2,1)S(1)}, u32[]{:S(2)}, u32[]{:S(2)}) collective-permute-start(bf16[1024,128]{1,0:T(8,128)(2,1)S(1)} %get-tuple-element.12), channel_id=1, source_target_pairs={{0,64},{64,128},{128,192},{1,65},{65,129},{129,193},{2,66},{66,130... | collective-permute-start | bytes 786440 | tf_op jit(solution)/shard_map/ppermute | solution.py:417
  111.5 2.9 %collective-permute-start.9 = (bf16[1024,128]{1,0:T(8,128)(2,1)S(1)}, bf16[1024,128]{1,0:T(8,128)(2,1)S(1)}, u32[]{:S(2)}, u32[]{:S(2)}) collective-permute-start(bf16[1024,128]{1,0:T(8,128)(2,1)S(1)} %get-tuple-element.12), channel_id=1, source_target_pairs={{64,0},{128,64},{192,128},{65,1},{129,65},{193,129},{66,2},{130,66... | collective-permute-start | bytes 786440 | tf_op jit(solution)/shard_map/ppermute | solution.py:417
  114.5 1.2 owned_stage.3.own_ref
  115.7 2.4 %collective-permute-done.8.low_ref = bf16[1024,128]{1,0:T(8,128)(2,1)S(1)} collective-permute-done((bf16[1024,128]{1,0:T(8,128)(2,1)S(1)}, bf16[1024,128]{1,0:T(8,128)(2,1)S(1)}, u32[]{:S(2)}, u32[]{:S(2)}) %collective-permute-start.8) | collective-permute-done | bytes 262176 | tf_op jit(solution)/shard_map/ppermute | solution.py:417
  118.1 2.8 %collective-permute-done.9.high_ref = bf16[1024,128]{1,0:T(8,128)(2,1)S(1)} collective-permute-done((bf16[1024,128]{1,0:T(8,128)(2,1)S(1)}, bf16[1024,128]{1,0:T(8,128)(2,1)S(1)}, u32[]{:S(2)}, u32[]{:S(2)}) %collective-permute-start.9) | collective-permute-done | bytes 262176 | tf_op jit(solution)/shard_map/ppermute | solution.py:417
  120.9 1.7 %stitch.3 = bf16[4,16,48,128]{3,2,1,0:T(8,128)(2,1)} custom-call(s32[4]{0:T(128)S(1)} %pad_add_fusion.scalar_ref, bf16[3072,128]{1,0:T(8,128)(2,1)S(1)} %owned_stage.3.own_ref, bf16[1024,128]{1,0:T(8,128)(2,1)S(1)} %collective-permute-done.8.low_ref, bf16[1024,128]{1,0:T(8,128)(2,1)S(1)} %collective-permute-done.9.high_ref), custom_call_target="tpu_custom_call" | custom-call | tf_op jit(solution)/shard_map/stitch/pallas_call | solution.py:279
  122.6 7.4 %all-to-all-start.1 = ((bf16[64,24,2,128]{3,2,1,0:T(2,128)(2,1)}), bf16[64,24,2,128]{3,2,1,0:T(2,128)(2,1)S(1)}, u32[]{:S(2)}, u32[]{:S(2)}) async-start(bf16[64,24,2,128]{3,2,1,0:T(2,128)(2,1)} %bitcast.26), calls=%async_computation.1 | async-start | bytes 1572864 | tf_op jit(solution)/shard_map/all_to_all | solution.py:502
  131.9 21.6 %all-to-all-done.1 = bf16[64,24,2,128]{3,2,1,0:T(2,128)(2,1)S(1)} async-done(((bf16[64,24,2,128]{3,2,1,0:T(2,128)(2,1)}), bf16[64,24,2,128]{3,2,1,0:T(2,128)(2,1)S(1)}, u32[]{:S(2)}, u32[]{:S(2)}) %all-to-all-start.1) | async-done | bytes 786464 | tf_op jit(solution)/shard_map/all_to_all | solution.py:502
  154.4 3.1 %azimuth_stage.1 = bf16[48,128,128]{2,1,0:T(8,128)(2,1)} custom-call(bf16[128,128]{1,0:T(8,128)(2,1)S(1)} %copy-done.4, bf16[256,256]{1,0:T(8,128)(2,1)S(1)} %copy-done.5, f32[2,64,128]{2,1,0:T(8,128)S(1)} %copy-done.7, f32[2,64,128]{2,1,0:T(8,128)S(1)} %copy-done.8, f32[2,64,128]{2,1,0:T(8,128)S(1)} %pad_maximum_fusion.3.filter_ref, ...), custom_call_target="tpu_custom_call" | custom-call | tf_op jit(solution)/shard_map/azimuth_stage/pallas_call | solution.py:401
  (65 shorter events, 8.5 us)
Async XLA Ops:
  2.0 29.1 %collective-permute-start = (bf16[2,64,1024]{2,1,0:T(8,128)(2,1)}, bf16[2,64,1024]{2,1,0:T(8,128)(2,1)S(1)}, u32[]{:S(2)}, u32[]{:S(2)}) collective-permute-start(bf16[2,64,1024]{2,1,0:T(8,128)(2,1)} %get-tuple-element.21), channel_id=1, source_target_pairs={{0,3},{1,0},{2,1},{3,2},{4,7},{5,4},{6,5},{7,6},{8,11},{9,8},{10,9... | collective-permute-start | bytes 786440 | tf_op jit(solution)/shard_map/ppermute | solution.py:478
  8.3 22.8 %collective-permute-start.1 = (bf16[2,64,1024]{2,1,0:T(8,128)(2,1)}, bf16[2,64,1024]{2,1,0:T(8,128)(2,1)S(1)}, u32[]{:S(2)}, u32[]{:S(2)}) collective-permute-start(bf16[2,64,1024]{2,1,0:T(8,128)(2,1)} %get-tuple-element.20), channel_id=1, source_target_pairs={{0,2},{1,3},{2,0},{3,1},{4,6},{5,7},{6,4},{7,5},{8,10},{9,11},{10,... | collective-permute-start | bytes 786440 | tf_op jit(solution)/shard_map/ppermute | solution.py:478
  9.2 21.9 %collective-permute-start.2 = (bf16[2,64,1024]{2,1,0:T(8,128)(2,1)S(1)}, bf16[2,64,1024]{2,1,0:T(8,128)(2,1)S(1)}, u32[]{:S(2)}, u32[]{:S(2)}) collective-permute-start(bf16[2,64,1024]{2,1,0:T(8,128)(2,1)S(1)} %get-tuple-element.19), channel_id=1, source_target_pairs={{0,1},{1,2},{2,3},{3,0},{4,5},{5,6},{6,7},{7,4},{8,9},{9,10},{10,1... | collective-permute-start | bytes 786440 | tf_op jit(solution)/shard_map/ppermute | solution.py:478
  21.3 9.7 %copy-start = (bf16[1,2,512,1024]{3,2,1,0:T(8,128)(2,1)S(1)}, bf16[1,2,512,1024]{3,2,1,0:T(8,128)(2,1)}, u32[]{:S(2)}) copy-start(bf16[1,2,512,1024]{3,2,1,0:T(8,128)(2,1)} %param.17) | copy-start | bytes 6291460
  21.3 9.7 %copy-start.3 = (bf16[128,256]{1,0:T(8,128)(2,1)S(1)}, bf16[128,256]{1,0:T(8,128)(2,1)}, u32[]{:S(2)}) copy-start(bf16[128,256]{1,0:T(8,128)(2,1)} %constant.149.clone.refs_7_) | copy-start | bytes 196612
  31.1 8.1 %copy-start.2 = (bf16[384,256]{1,0:T(8,128)(2,1)S(1)}, bf16[384,256]{1,0:T(8,128)(2,1)}, u32[]{:S(2)}) copy-start(bf16[384,256]{1,0:T(8,128)(2,1)} %constant.150.clone.table_ref) | copy-start | bytes 589828
  33.3 8.3 %collective-permute-start.3 = (bf16[1024,128]{1,0:T(8,128)(2,1)S(1)}, bf16[1024,128]{1,0:T(8,128)(2,1)S(1)}, u32[]{:S(2)}, u32[]{:S(2)}) collective-permute-start(bf16[1024,128]{1,0:T(8,128)(2,1)S(1)} %get-tuple-element.10), channel_id=1, source_target_pairs={{0,64},{64,128},{128,192},{1,65},{65,129},{129,193},{2,66},{66,130... | collective-permute-start | bytes 786440 | tf_op jit(solution)/shard_map/ppermute | solution.py:417
  36.7 8.3 %collective-permute-start.4 = (bf16[1024,128]{1,0:T(8,128)(2,1)S(1)}, bf16[1024,128]{1,0:T(8,128)(2,1)S(1)}, u32[]{:S(2)}, u32[]{:S(2)}) collective-permute-start(bf16[1024,128]{1,0:T(8,128)(2,1)S(1)} %get-tuple-element.10), channel_id=1, source_target_pairs={{64,0},{128,64},{192,128},{65,1},{129,65},{193,129},{66,2},{130,66... | collective-permute-start | bytes 786440 | tf_op jit(solution)/shard_map/ppermute | solution.py:417
  46.7 23.7 %copy-start.11 = (f32[1,128,128]{2,1,0:T(8,128)S(1)}, f32[1,128,128]{2,1,0:T(8,128)}, u32[]{:S(2)}) copy-start(f32[1,128,128]{2,1,0:T(8,128)} %get-tuple-element.35) | copy-start | bytes 196612
  46.7 76.0 %all-to-all-start = ((bf16[64,24,2,128]{3,2,1,0:T(2,128)(2,1)}), bf16[64,24,2,128]{3,2,1,0:T(2,128)(2,1)S(1)}, u32[]{:S(2)}, u32[]{:S(2)}) async-start(bf16[64,24,2,128]{3,2,1,0:T(2,128)(2,1)} %bitcast.21), calls=%async_computation | async-start | bytes 1572864 | tf_op jit(solution)/shard_map/all_to_all | solution.py:502
  61.8 31.5 %collective-permute-start.5 = (bf16[2,64,1024]{2,1,0:T(8,128)(2,1)S(1)}, bf16[2,64,1024]{2,1,0:T(8,128)(2,1)S(1)}, u32[]{:S(2)}, u32[]{:S(2)}) collective-permute-start(bf16[2,64,1024]{2,1,0:T(8,128)(2,1)S(1)} %get-tuple-element.18), channel_id=1, source_target_pairs={{0,3},{1,0},{2,1},{3,2},{4,7},{5,4},{6,5},{7,6},{8,11},{9,8},{10,9... | collective-permute-start | bytes 786440 | tf_op jit(solution)/shard_map/ppermute | solution.py:478
  65.8 35.1 %collective-permute-start.6 = (bf16[2,64,1024]{2,1,0:T(8,128)(2,1)S(1)}, bf16[2,64,1024]{2,1,0:T(8,128)(2,1)S(1)}, u32[]{:S(2)}, u32[]{:S(2)}) collective-permute-start(bf16[2,64,1024]{2,1,0:T(8,128)(2,1)S(1)} %get-tuple-element.17), channel_id=1, source_target_pairs={{0,2},{1,3},{2,0},{3,1},{4,6},{5,7},{6,4},{7,5},{8,10},{9,11},{10,... | collective-permute-start | bytes 786440 | tf_op jit(solution)/shard_map/ppermute | solution.py:478
  67.9 36.7 %collective-permute-start.7 = (bf16[2,64,1024]{2,1,0:T(8,128)(2,1)S(1)}, bf16[2,64,1024]{2,1,0:T(8,128)(2,1)S(1)}, u32[]{:S(2)}, u32[]{:S(2)}) collective-permute-start(bf16[2,64,1024]{2,1,0:T(8,128)(2,1)S(1)} %get-tuple-element.16), channel_id=1, source_target_pairs={{0,1},{1,2},{2,3},{3,0},{4,5},{5,6},{6,7},{7,4},{8,9},{9,10},{10,1... | collective-permute-start | bytes 786440 | tf_op jit(solution)/shard_map/ppermute | solution.py:478
  104.6 1.6 %copy-start.1 = (bf16[1,2,512,1024]{3,2,1,0:T(8,128)(2,1)S(1)}, bf16[1,2,512,1024]{3,2,1,0:T(8,128)(2,1)}, u32[]{:S(2)}) copy-start(bf16[1,2,512,1024]{3,2,1,0:T(8,128)(2,1)} %param.17) | copy-start | bytes 6291460
  108.4 9.7 %collective-permute-start.8 = (bf16[1024,128]{1,0:T(8,128)(2,1)S(1)}, bf16[1024,128]{1,0:T(8,128)(2,1)S(1)}, u32[]{:S(2)}, u32[]{:S(2)}) collective-permute-start(bf16[1024,128]{1,0:T(8,128)(2,1)S(1)} %get-tuple-element.12), channel_id=1, source_target_pairs={{0,64},{64,128},{128,192},{1,65},{65,129},{129,193},{2,66},{66,130... | collective-permute-start | bytes 786440 | tf_op jit(solution)/shard_map/ppermute | solution.py:417
  111.5 9.4 %collective-permute-start.9 = (bf16[1024,128]{1,0:T(8,128)(2,1)S(1)}, bf16[1024,128]{1,0:T(8,128)(2,1)S(1)}, u32[]{:S(2)}, u32[]{:S(2)}) collective-permute-start(bf16[1024,128]{1,0:T(8,128)(2,1)S(1)} %get-tuple-element.12), channel_id=1, source_target_pairs={{64,0},{128,64},{192,128},{65,1},{129,65},{193,129},{66,2},{130,66... | collective-permute-start | bytes 786440 | tf_op jit(solution)/shard_map/ppermute | solution.py:417
  115.7 14.3 %copy-start.12 = (f32[8192]{0:T(1024)S(1)}, f32[8192]{0:T(1024)}, u32[]{:S(2)}) copy-start(f32[8192]{0:T(1024)} %param.21) | copy-start | bytes 98308
  122.6 8.7 %copy-start.4 = (bf16[128,128]{1,0:T(8,128)(2,1)S(1)}, bf16[128,128]{1,0:T(8,128)(2,1)}, u32[]{:S(2)}) copy-start(bf16[128,128]{1,0:T(8,128)(2,1)} %constant.151.clone.first_ref) | copy-start | bytes 98308
  122.6 8.7 %copy-start.9 = (f32[2,64,128]{2,1,0:T(8,128)S(1)}, f32[2,64,128]{2,1,0:T(8,128)}, u32[]{:S(2)}) copy-start(f32[2,64,128]{2,1,0:T(8,128)} %constant.152.clone.twist_ref) | copy-start | bytes 196612
  122.6 30.9 %all-to-all-start.1 = ((bf16[64,24,2,128]{3,2,1,0:T(2,128)(2,1)}), bf16[64,24,2,128]{3,2,1,0:T(2,128)(2,1)S(1)}, u32[]{:S(2)}, u32[]{:S(2)}) async-start(bf16[64,24,2,128]{3,2,1,0:T(2,128)(2,1)} %bitcast.26), calls=%async_computation.1 | async-start | bytes 1572864 | tf_op jit(solution)/shard_map/all_to_all | solution.py:502
  130.5 23.9 %copy-start.5 = (bf16[256,256]{1,0:T(8,128)(2,1)S(1)}, bf16[256,256]{1,0:T(8,128)(2,1)}, u32[]{:S(2)}) copy-start(bf16[256,256]{1,0:T(8,128)(2,1)} %constant.153.clone.fore_ref) | copy-start | bytes 393220
  130.5 23.8 %copy-start.6 = (bf16[256,256]{1,0:T(8,128)(2,1)S(1)}, bf16[256,256]{1,0:T(8,128)(2,1)}, u32[]{:S(2)}) copy-start(bf16[256,256]{1,0:T(8,128)(2,1)} %constant.156.clone.back_ref) | copy-start | bytes 393220
  130.5 23.8 %copy-start.7 = (f32[2,64,128]{2,1,0:T(8,128)S(1)}, f32[2,64,128]{2,1,0:T(8,128)}, u32[]{:S(2)}) copy-start(f32[2,64,128]{2,1,0:T(8,128)} %constant.154.clone.twist_ref) | copy-start | bytes 196612
  130.5 23.8 %copy-start.8 = (f32[2,64,128]{2,1,0:T(8,128)S(1)}, f32[2,64,128]{2,1,0:T(8,128)}, u32[]{:S(2)}) copy-start(f32[2,64,128]{2,1,0:T(8,128)} %constant.155.clone.back_twist_ref) | copy-start | bytes 196612
  130.5 23.8 %copy-start.10 = (bf16[128,128]{1,0:T(8,128)(2,1)S(1)}, bf16[128,128]{1,0:T(8,128)(2,1)}, u32[]{:S(2)}) copy-start(bf16[128,128]{1,0:T(8,128)(2,1)} %constant.157.clone.last_ref) | copy-start | bytes 98308
